TPU v7x, 1024 devices: a whole 8x8x8 slice. The times are simulated.
1024 devices in a mesh: grp: 64 (over y_lo, z, core), blk: 16 (over y_hi, x).
Axes of the slice: x: 8, y: 8 (y_hi: 2, y_lo: 4; y = y_hi * 4 + y_lo), z: 8, core: 2. Of those that a mesh axis runs over, the one named last changes fastest.
Arguments:
- integrals: bfloat16 [8, 128, 128, 128], P(None, 'blk'), may hold values from -0.5 to 0.5
- doubles: bfloat16 [64, 128, 128], P('blk'), may hold values from -0.0059814453 to 0.0059814453
- coulomb: bfloat16 [64, 128, 128], P('blk'), may hold values from -0.1796875 to 0.1796875
- singles: float32 [8, 128], P(None, 'blk'), may hold values from -0.18 to 0.18
- occ_energy: float32 [8], replicated, may hold values from -2 to -0.5
- vir_energy: float32 [128], replicated, may hold values from 0.3 to 3
- triplets: int32 [64, 16, 3], P('grp'), may hold values from 0 to 7
- tile_count: int32 [64], P('grp'), may hold values from 1 to 16, as said below
Outputs:
- triplet_energy: float32 [64, 16], P('grp')
- mean_energy: float32 [], replicated
Inputs may be any that keep to these rules, and one draw needn't show every extreme that they name: `tile_count`: slots with an index below a group's count are live; some group has all 16 slots live.
All inputs are finite; a program needn't handle non-finite values.
Results may differ from a plain program's by a relative error of at most 0.0003.
Values may be sent and summed in bfloat16 or wider, within the bound.
No kernel may reach another device: no remote copies, remote signals or barrier semaphores. Data moves between devices by JAX's collectives and lax.ppermute only.
A program may use at most 64 MiB of HBM per device.

v0:
```python
import jax
import jax.numpy as jnp
from jax import lax
from jax.sharding import PartitionSpec as P


def sent_together(arrays, axis, dim, along):
    both = jnp.concatenate(arrays, axis=along)
    filled, at, outs = (lax.all_gather(both, axis, axis=dim, tiled=True), 0, [])
    for a in arrays:
        outs.append(lax.slice_in_dim(filled, at, at + a.shape[along], axis=along))
        at += a.shape[along]
    return tuple(outs)


def sent_to_all(shard, axis):
    copies = jnp.broadcast_to(shard, (lax.axis_size(axis), *shard.shape))
    return lax.all_to_all(copies, axis, split_axis=0, concat_axis=0, tiled=True)


def taken_together(shard, axis):
    return sent_to_all(shard, axis).sum(axis=0)


def select_blocks(pieces, pair_kj, pair_jk):
    doubles_piece = pieces[0]
    coulomb_piece = pieces[1]
    row_count = doubles_piece.shape[0]
    owned = jnp.arange(row_count, dtype=jnp.int32)
    pick_kj = (pair_kj[:, None] == owned[None, :]).astype(jnp.bfloat16)
    pick_jk = (pair_jk[:, None] == owned[None, :]).astype(jnp.bfloat16)
    flat_doubles = doubles_piece.reshape(row_count, -1)
    flat_coulomb = coulomb_piece.reshape(row_count, -1)
    return (
        jnp.dot(pick_kj, flat_doubles, preferred_element_type=jnp.float32),
        jnp.dot(pick_jk, flat_doubles, preferred_element_type=jnp.float32),
        jnp.dot(pick_jk, flat_coulomb, preferred_element_type=jnp.float32),
    )


def body(integrals, doubles, coulomb, singles, occ_energy, vir_energy, triplets, tile_count):
    occupied = integrals.shape[0]
    width_block = integrals.shape[1]
    width = integrals.shape[3]
    slots = triplets.shape[1]
    second_list = triplets[0, :, 1]
    third_list = triplets[0, :, 2]
    pair_kj = third_list * occupied + second_list
    pair_jk = second_list * occupied + third_list
    picked = select_blocks(sent_together((doubles, coulomb), "blk", 0, 1), pair_kj, pair_jk)
    doubles_kj = picked[0].astype(jnp.bfloat16).reshape(slots, width, width)
    doubles_jk = picked[1].astype(jnp.bfloat16).reshape(slots, width, width)
    coupling_all = picked[2].reshape(slots, width, width)
    block_offset = lax.axis_index("blk") * width_block
    vir_block = lax.dynamic_slice_in_dim(vir_energy, block_offset, width_block)
    vir_sums = vir_block[:, None, None] + vir_energy[None, :, None] + vir_energy[None, None, :]
    slot_ids = jnp.arange(slots, dtype=jnp.int32)
    contract = (((1,), (1,)), ((), ()))

    def slot_step(slot_index, energies):
        first_occ = triplets[0, slot_index, 0]
        second_occ = triplets[0, slot_index, 1]
        third_occ = triplets[0, slot_index, 2]
        slab = lax.dynamic_index_in_dim(integrals, first_occ, 0, False).reshape(
            width_block * width, width
        )
        block_kj = lax.dynamic_index_in_dim(doubles_kj, slot_index, 0, False)
        block_jk = lax.dynamic_index_in_dim(doubles_jk, slot_index, 0, False)
        coupling = lax.dynamic_index_in_dim(coupling_all, slot_index, 0, False)
        first = lax.dot_general(
            slab, block_kj, contract, preferred_element_type=jnp.float32
        ).reshape(width_block, width, width)
        second = lax.dot_general(
            slab, block_jk, contract, preferred_element_type=jnp.float32
        ).reshape(width_block, width, width)
        connected = first + jnp.transpose(second, (0, 2, 1))
        amp_row = lax.dynamic_index_in_dim(singles, first_occ, 0, False)
        full = connected + amp_row[:, None, None] * coupling[None, :, :]
        occ_sum = occ_energy[first_occ] + occ_energy[second_occ] + occ_energy[third_occ]
        denominator = occ_sum - vir_sums
        value = jnp.sum(full * full / denominator)
        value = jnp.where(slot_index < tile_count[0], value, jnp.float32(0.0))
        return energies + jnp.where(slot_ids == slot_index, value, jnp.float32(0.0))

    energies = lax.fori_loop(0, slots, slot_step, jnp.zeros((slots,), jnp.float32))
    trip_energy = taken_together(energies, "blk")
    grand_total = taken_together(jnp.sum(trip_energy), "grp")
    mean_energy = grand_total / (lax.axis_size("grp") * slots)
    return (trip_energy.reshape(1, slots), mean_energy)


def solution(mesh):
    in_specs = (
        P(None, "blk", None, None),
        P("blk", None, None),
        P("blk", None, None),
        P(None, "blk"),
        P(),
        P(),
        P("grp", None, None),
        P("grp"),
    )
    out_specs = (P("grp", None), P())
    return jax.shard_map(body, mesh=mesh, in_specs=in_specs, out_specs=out_specs, check_vma=False)
```

profile of v0, /device:TPU:1, one launch (start us, length us, event | category | flops | bytes accessed | tf_op | source)
XLA Modules:
  0.0 435.8 jit_solution(17486125132318887130)
XLA Ops:
  7.2 1.7 pad_maximum_fusion
  11.1 148.1 %all-gather.2.cloned.1.call-done = bf16[64,256,128]{2,1,0:T(8,128)(2,1)} async-done(((bf16[4,256,128]{2,1,0:T(8,128)(2,1)}), bf16[64,256,128]{2,1,0:T(8,128)(2,1)}) %all-gather.2.cloned.1.call-update) | async-done | bytes 4194320 | tf_op jit(solution)/shard_map/all_gather | solution.py:9
  159.2 2.7 fusion.43
  161.9 1.2 fusion.29
  164.6 1.2 fusion.24
  165.9 218.8 %while.14 = (s32[]{:T(128)}, f32[16]{0:T(128)S(1)}, s32[1]{0:T(128)}, s32[1,16,3]{1,0,2:T(1,128)S(1)}, bf16[8,8,128,128]{3,2,1,0:T(8,128)(2,1)}, /*index=5*/bf16...) while((s32[]{:T(128)}, f32[16]{0:T(128)S(1)}, ...), condition=%wide.region_2.3_spmd.clone, body=%wide.region_0.2_spmd.clone.sunk | while | flops 68157512 | bytes 1841247 | solution.py:85
  177.1 1.9 fusion.60
  190.8 1.9 fusion.60
  204.4 1.9 fusion.60
  218.1 1.9 fusion.60
  231.8 1.9 fusion.60
  245.5 1.9 fusion.60
  259.1 1.9 fusion.60
  272.8 1.9 fusion.60
  286.5 1.9 fusion.60
  300.2 1.9 fusion.60
  313.8 1.9 fusion.60
  327.5 1.9 fusion.60
  341.2 1.9 fusion.60
  354.9 1.9 fusion.60
  368.5 1.9 fusion.60
  382.2 1.9 fusion.60
  384.7 15.4 %all_to_all.12 = f32[16,1,16]{2,1,0:T(1,128)S(1)} all-to-all(f32[16,1,16]{2,1,0:T(1,128)S(1)} %broadcast_in_dim.33), channel_id=1, replica_groups=mesh['grp'=64,'blk'=16] {'blk'}, dimensions={0} | all-to-all | bytes 2048 | tf_op jit(solution)/shard_map/all_to_all | solution.py:18
  401.4 25.2 %all_to_all.13 = f32[64,1,1]{2,1,0:T(1,128)S(1)} all-to-all(f32[64,1,1]{2,1,0:T(1,128)S(1)} %broadcast_in_dim.34), channel_id=1, replica_groups=mesh['grp'=64,'blk'=16] {'grp'}, dimensions={0} | all-to-all | bytes 512 | tf_op jit(solution)/shard_map/all_to_all | solution.py:18
  (115 shorter events, 56.5 us)
Async XLA Ops:
  7.2 152.0 %all-gather.2.cloned.1.call-start = ((), (), s32[]{:S(2)}) async-start(), calls=%async_computation.2 | async-start | bytes 4456448 | tf_op jit(solution)/shard_map/all_gather | solution.py:9
  164.5 1.4 copy-start
  164.5 1.4 copy-start.1
  164.5 1.4 copy-start.2
Sparse Core Ops, SparseCore 0:
  12.3 146.7 all-gather.1
where the time goes:
time: 440 us; the launch traced here: 436 us
  waiting for transfers between devices  148 us (34%)
  loops' own time  138 us (31%)
  matrix products  52.4 us (12%)
  blocking collectives  40.6 us (9%)
  local copies, waits for them, and re-layouts  36.2 us (8%)
  between operations  15.9 us (4%)
  other arithmetic  4.57 us (1%)
    all_gather x1, waiting for transfers between devices, sent_together(): filled, at, outs = (lax.all_gather(both, axis, axis=dim, tiled=True), 0, [])  148 us
    another operation x1, loops' own time, body(): lax.fori_loop(0, slots, slot_step, jnp.zeros((slots,), jnp.float32))  138 us
    all_to_all x2, blocking collectives, sent_to_all(): return lax.all_to_all(copies, axis, split_axis=0, concat_axis=0, tiled=True)  40.6 us
    dot_general x16, matrix products, slot_step(): lax.dot_general(slab, block_jk, contract, preferred_element_type=jnp.floa...  29.9 us
    dot_general x16, matrix products, slot_step(): lax.dot_general(slab, block_kj, contract, preferred_element_type=jnp.floa...  18.8 us
    mul x16, local copies, waits for them, and re-layouts, slot_step(): full = connected + amp_row[:, None, None] * coupling[None, :, :]  11.2 us
    dynamic_slice x16, local copies, waits for them, and re-layouts, slot_step(): occ_energy[third_occ]  9.94 us
    dynamic_slice x16, local copies, waits for them, and re-layouts, slot_step(): third_occ = triplets[0, slot_index, 2]  9.85 us
  transfers between devices with their start and end apart: 1, of which 1 were waited for; matrix products, arithmetic and copies ran while one was open for 0% of the time, Pallas kernels for 0%

commit v1 on v0

v1 whole, which is shorter than its diff:
```python
import functools

import jax
import jax.numpy as jnp
import numpy as np
from jax import lax
from jax.experimental import pallas as pl
from jax.experimental.pallas import tpu as pltpu
from jax.sharding import Mesh
from jax.sharding import PartitionSpec as P

AXES = ("yl", "z", "c", "yh", "x")
SIZES = (4, 8, 2, 2, 8)
GRP = ("yl", "z", "c")
BLK = ("yh", "x")
PLANE = ("yh", "yl", "x")
STACK = ("z", "c")
NO = 8
SMALL = pltpu.CompilerParams(vmem_limit_bytes=8 * 1024 * 1024)


def device_at(yl, z, c, yh, x):
    return ((((yl * 8) + z) * 2 + c) * 2 + yh) * 8 + x


def pair_of(yl, z, c, yh, x):
    row_yh = yh ^ c
    row_x = (x - z - 4 * c) & 7
    second = row_yh * 4 + (row_x >> 1)
    third = (row_x & 1) * 4 + ((row_x >> 1) ^ yl) % 4
    return row_yh, row_x, second, third


def routes():
    straight, swapped = [], []
    for yl, z, c, yh, x in np.ndindex(*SIZES):
        row_yh, row_x, second, third = pair_of(yl, z, c, yh, x)
        here = device_at(yl, z, c, yh, x)
        from_yl = yl ^ (2 * int(row_yh != yh))
        straight.append((device_at(from_yl, z, c, row_yh, row_x), here))
        owner = third * 2 + second // 4
        from_yl = yl ^ (2 * int(owner // 8 != yh))
        swapped.append((device_at(from_yl, z, c, owner // 8, owner % 8), here))
    return straight, swapped


def recip_kernel(shift_ref, sums_ref, out_ref):
    sums = sums_ref[...]

    def one_row(r, carry):
        out_ref[pl.ds(r, 1)] = 1.0 / (shift_ref[pl.ds(r, 1), :] - sums)[None]
        return carry

    lax.fori_loop(0, out_ref.shape[0], one_row, 0, unroll=2)


def energy_kernel(ints_ref, rows_ref, swap_ref, recip_ref, amps_ref, info_ref, out_ref, sums_ref):
    occupied, width_block, width, _ = ints_ref.shape
    block_jk = rows_ref[0]
    coupling = rows_ref[1].astype(jnp.float32)
    block_kj = swap_ref[...]
    contract = (((1,), (1,)), ((), ()))

    def one_occ(i, carry):
        total = jnp.zeros((8, width), jnp.float32)
        for a in range(width_block):
            slab = ints_ref[i, a]
            left = jnp.concatenate([slab, block_jk], axis=1)
            right = jnp.concatenate([block_kj, slab], axis=1)
            connected = lax.dot_general(left, right, contract, preferred_element_type=jnp.float32)
            amp = amps_ref[pl.ds(i * width_block + a, 1), :]
            full = connected + amp * coupling
            value = full * full * recip_ref[i * width_block + a]
            total = total + jnp.sum(value.reshape(width // 8, 8, width), axis=0)
        sums_ref[pl.ds(i, 1), :] = jnp.sum(total, axis=0, keepdims=True)
        return carry

    lax.fori_loop(0, occupied, one_occ, 0)
    energies = jnp.sum(sums_ref[...], axis=1, keepdims=True)
    sub = lax.broadcasted_iota(jnp.int32, (occupied, 128), 0)
    lane = lax.broadcasted_iota(jnp.int32, (occupied, 128), 1)
    row = jnp.sum(jnp.where(sub == lane, energies, 0.0), axis=0, keepdims=True)
    out_ref[...] = jnp.broadcast_to(row + info_ref[...], out_ref.shape)


def table_kernel(in_ref, out_ref):
    got = in_ref[...]
    lane = lax.broadcasted_iota(jnp.int32, got.shape, 1).astype(jnp.float32)
    pick = jnp.where(lane < 64.0, got[:, 16:17], got[:, 17:18] + 64.0) == lane
    both = lax.dot_general(
        got,
        pick.astype(jnp.float32),
        (((0,), (0,)), ((), ())),
        precision=lax.Precision.HIGHEST,
        preferred_element_type=jnp.float32,
    )
    low = lax.broadcasted_iota(jnp.int32, (8, 128), 1) < 64
    packed = jnp.where(low, both[0:8], both[8:16])
    peers = out_ref.shape[0] // 8
    out_ref[...] = jnp.broadcast_to(packed[None], (peers, 8, 128)).reshape(peers * 8, 128)


def final_kernel(in_ref, first_ref, pair_ref, trip_ref, mean_ref):
    peers = in_ref.shape[0] // 8
    table = jnp.sum(in_ref[...].reshape(peers, 8, 128), axis=0)
    counts = pltpu.roll(table, 64, 1)
    low = lax.broadcasted_iota(jnp.int32, (8, 128), 1) < 64
    weighted = jnp.where(low, table * counts, 0.0)
    mean_ref[...] = jnp.sum(jnp.sum(weighted, axis=0, keepdims=True), axis=1, keepdims=True) / 1024.0
    chosen = jnp.zeros((16, 128), jnp.float32)
    for i in range(8):
        chosen = chosen + first_ref[:, i:i + 1] * table[i:i + 1, :]
    values = jnp.sum(chosen * pair_ref[...], axis=1, keepdims=True)
    sub = lax.broadcasted_iota(jnp.int32, (16, 128), 0)
    lane = lax.broadcasted_iota(jnp.int32, (16, 128), 1)
    row = jnp.sum(jnp.where(sub == lane, values, 0.0), axis=0, keepdims=True)
    trip_ref[...] = row[:, :16]


def vmem(count):
    return [pl.BlockSpec(memory_space=pltpu.VMEM)] * count


def kept(*arrays):
    return [pltpu.with_memory_space_constraint(a, pltpu.VMEM) for a in arrays]


def body(integrals, doubles, coulomb, singles, occ_energy, vir_energy, triplets, tile_count):
    occupied, width_block, width, _ = integrals.shape
    slots = triplets.shape[1]
    yl, z, c, yh, x = (lax.axis_index(axis) for axis in AXES)
    place = yh * 8 + x
    straight, swapped = routes()

    low_bits = (place >> 1) & 3
    target_yl = yl ^ (2 * c)
    swap_yl = yl ^ (2 * (yh ^ (x & 1) ^ c))
    row_straight = low_bits ^ target_yl
    row_swapped = low_bits ^ swap_yl
    take = functools.partial(lax.dynamic_index_in_dim, axis=0, keepdims=False)
    sent = jnp.stack([take(doubles, row_straight), take(coulomb, row_straight)])
    rows = lax.ppermute(sent, AXES, straight)
    swap = lax.ppermute(take(doubles, row_swapped), AXES, swapped)

    _, _, second, third = pair_of(yl, z, c, yh, x)
    own_pair = second * NO + third
    vir_block = lax.dynamic_slice_in_dim(vir_energy, place * width_block, width_block)
    occ_sums = occ_energy + occ_energy[second] + occ_energy[third]
    shifts = (occ_sums[:, None] - vir_block[None, :]).reshape(-1)
    vir_sums = vir_energy[:, None] + vir_energy[None, :]
    shifts = jnp.broadcast_to(shifts[:, None], (occupied * width_block, width))
    recip = pl.pallas_call(
        recip_kernel,
        out_shape=pltpu.VMEM((occupied * width_block, width, width), jnp.float32),
        in_specs=vmem(2),
        out_specs=vmem(1)[0],
        compiler_params=SMALL,
        name="reciprocals",
    )(*kept(shifts, vir_sums))
    amps = jnp.broadcast_to(singles.reshape(-1, 1), (occupied * width_block, width))

    lane = jnp.arange(128, dtype=jnp.int32)
    live = jnp.arange(slots, dtype=jnp.int32) < tile_count[0]
    firsts = triplets[0, :, 0]
    pairs = triplets[0, :, 1] * NO + triplets[0, :, 2]
    first_hot = ((firsts[:, None] == lane[None, :]) & live[:, None]).astype(jnp.float32)
    pair_hot = (pairs[:, None] == lane[None, :]).astype(jnp.float32)
    my_first = firsts[place]
    my_pair = pairs[place]
    my_live = place < tile_count[0]
    info = jnp.where((lane == my_first + 8) & my_live, 1.0, 0.0)
    info = jnp.where(lane == 16, own_pair.astype(jnp.float32), info)
    info = jnp.where(lane == 17, my_pair.astype(jnp.float32), info)

    recip, amps, info, first_hot, pair_hot = lax.optimization_barrier((recip, amps, info, first_hot, pair_hot))
    message = pl.pallas_call(
        energy_kernel,
        out_shape=pltpu.VMEM((64, 128), jnp.float32),
        in_specs=vmem(6),
        out_specs=vmem(1)[0],
        scratch_shapes=[pltpu.VMEM((occupied, width), jnp.float32)],
        compiler_params=SMALL,
        name="energies",
    )(*kept(integrals, rows, swap, recip, amps, info[None]))
    message = lax.all_to_all(message, PLANE, 0, 0, tiled=True)
    tables = pl.pallas_call(
        table_kernel,
        out_shape=pltpu.VMEM((128, 128), jnp.float32),
        in_specs=vmem(1),
        out_specs=vmem(1)[0],
        compiler_params=SMALL,
        name="table",
    )(*kept(message))
    tables = lax.all_to_all(tables, STACK, 0, 0, tiled=True)
    trip, mean = pl.pallas_call(
        final_kernel,
        out_shape=(
            jax.ShapeDtypeStruct((1, slots), jnp.float32),
            jax.ShapeDtypeStruct((1, 1), jnp.float32),
        ),
        in_specs=vmem(3),
        out_specs=tuple(vmem(2)),
        compiler_params=SMALL,
        name="lookup",
    )(*kept(tables, first_hot, pair_hot))
    return trip, mean.reshape(())


def solution(mesh):
    fine = Mesh(mesh.devices.reshape(SIZES), AXES)
    in_specs = (
        P(None, BLK, None, None),
        P(BLK, None, None),
        P(BLK, None, None),
        P(None, BLK),
        P(),
        P(),
        P(GRP, None, None),
        P(GRP),
    )
    out_specs = (P(GRP, None), P())
    return jax.shard_map(body, mesh=fine, in_specs=in_specs, out_specs=out_specs, check_vma=False)
```

time: 440 us -> 74.5 us (0.17)
  waiting for transfers between devices: 148 us -> 0.01 us
  loops' own time: 138 us -> 0 us
  matrix products: 52.4 us -> 0 us
  local copies, waits for them, and re-layouts: 36.2 us -> 4.75 us
  between operations: 15.9 us -> 1.44 us
  starting transfers between devices: 0.04 us -> 14.2 us
    all_gather x1 -> x0, waiting for transfers between devices: 148 us -> none  [sent_together(): filled, at, outs = (lax.all_gather(both, axis, axis=dim, tiled=True), 0, [])]
    another operation x1 -> x0, loops' own time: 138 us -> none  [body(): lax.fori_loop(0, slots, slot_step, jnp.zeros((slots,), jnp.float32))]
    dot_general x35 -> x0, matrix products: 52.4 us -> none  [the longest x16 29.9 us: slot_step(): lax.dot_general(slab, block_jk, contract, preferred_element_type=jnp.floa...]
    dynamic_slice x49 -> x3, local copies, waits for them, and re-layouts: 21.4 us -> 2.06 us  [the longest x1 1.32 us: body(): occ_sums = occ_energy + occ_energy[second] + occ_energy[third]]
    ppermute x0 -> x2, starting transfers between devices: none -> 14.2 us  [the longest x1 12.2 us: body(): rows = lax.ppermute(sent, AXES, straight)]
    mul x16 -> x0, local copies, waits for them, and re-layouts: 11.2 us -> none  [slot_step(): full = connected + amp_row[:, None, None] * coupling[None, :, :]]
  transfers between devices with their start and end apart: 1 -> 2, of which waited for: 1 -> 0; matrix products, arithmetic and copies ran while one was open for 0% -> 12% of each run, Pallas kernels for 0% -> 1%
where the time goes in v1:
time: 74.5 us; the launch traced here: 74.1 us
  blocking collectives  43.9 us (59%)
  starting transfers between devices  14.2 us (19%)
  other arithmetic  5.5 us (7%)
  local copies, waits for them, and re-layouts  4.75 us (6%)
  Pallas kernels  4.37 us (6%)
  between operations  1.44 us (2%)
    all_to_all x1, blocking collectives, body(): tables = lax.all_to_all(tables, STACK, 0, 0, tiled=True)  23.4 us
    all_to_all x1, blocking collectives, body(): message = lax.all_to_all(message, PLANE, 0, 0, tiled=True)  20.5 us
    ppermute x1, starting transfers between devices, body(): rows = lax.ppermute(sent, AXES, straight)  12.2 us
    pallas_call x1, Pallas kernels, body(): pl.pallas_call(energy_kernel, out_shape=pltpu.VMEM((64, 128), jnp.float32...  2.59 us
    add x1, other arithmetic, body(): occ_sums = occ_energy + occ_energy[second] + occ_energy[third]  1.95 us
    ppermute x1, starting transfers between devices, body(): swap = lax.ppermute(take(doubles, row_swapped), AXES, swapped)  1.92 us
  transfers between devices with their start and end apart: 2, of which 0 were waited for; matrix products, arithmetic and copies ran while one was open for 12% of the time, Pallas kernels for 1%

profile of v1, /device:TPU:1, one launch (start us, length us, event | category | flops | bytes accessed | tf_op | source)
XLA Modules:
  0.0 74.1 jit_solution(4130810710069148447)
XLA Ops:
  0.6 0.0 copy-start
  0.7 0.9 %copy-done = bf16[4,128,128]{2,1,0:T(8,128)(2,1)S(1)} copy-done((bf16[4,128,128]{2,1,0:T(8,128)(2,1)S(1)}, bf16[4,128,128]{2,1,0:T(8,128)(2,1)}, u32[]{:S(2)}) %copy-start) | copy-done | bytes 131096
  1.5 0.8 %dynamic-slice_bitcast_fusion = (bf16[128,128]{1,0:T(8,128)(2,1)S(1)}, bf16[1,128,128]{2,1,0:T(8,128)(2,1)S(1)}) fusion(bf16[4,128,128]{2,1,0:T(8,128)(2,1)} %param.9, s32[]{:T(128)S(6)} %select_n.41, s32[]{:T(128)S(6)} %select_n.40), kind=kLoop, calls=%fused_computation.2 | loop fusion | bytes 131080 | tf_op jit(solution)/shard_map/jit(dynamic_index_in_dim)/squeeze | solution.py:143
  2.4 12.2 %collective-permute-start = (bf16[2,128,128]{2,1,0:T(8,128)(2,1)S(1)}, bf16[2,128,128]{2,1,0:T(8,128)(2,1)S(1)}, u32[]{:S(2)}, u32[]{:S(2)}) collective-permute-start(bf16[2,128,128]{2,1,0:T(8,128)(2,1)S(1)} %pad_maximum_fusion), channel_id=1, source_target_pairs={{0,0},{1,1},{2,2},{3,3},{4,4},{5,5},{6,6},{7,7},{8,8},{9,9},{10,10... | collective-permute-start | bytes 196616 | tf_op jit(solution)/shard_map/ppermute | solution.py:142
  14.6 1.9 %collective-permute-start.1 = (bf16[128,128]{1,0:T(8,128)(2,1)S(1)}, bf16[128,128]{1,0:T(8,128)(2,1)S(1)}, u32[]{:S(2)}, u32[]{:S(2)}) collective-permute-start(bf16[128,128]{1,0:T(8,128)(2,1)S(1)} %get-tuple-element.16), channel_id=1, source_target_pairs={{0,0},{520,1},{2,2},{522,3},{4,4},{524,5},{6,6},{526,7},{513,8},{9... | collective-permute-start | bytes 98312 | tf_op jit(solution)/shard_map/ppermute | solution.py:143
  16.6 0.8 %broadcast_add_fusion.sums_ref = f32[128,128]{1,0:T(8,128)S(1)} fusion(f32[128]{0:T(128)} %param.13), kind=kLoop, calls=%fused_computation.1 | loop fusion | flops 16384 | bytes 66048 | tf_op jit(solution)/shard_map/add | solution.py:150
  17.4 0.7 dynamic_slice.30
  18.8 0.7 slice_bitcast_fusion
  19.5 1.3 %fusion.3 = (f32[1]{0:T(128)}, f32[1]{0:T(128)}) fusion(f32[8]{0:T(128)} %param.12, s32[]{:T(128)S(6)} %select_n.42, s32[]{:T(128)S(6)} %select_n.44), kind=kLoop, calls=%fused_computation.20 | loop fusion | bytes 24 | tf_op jit(solution)/shard_map/dynamic_slice | solution.py:148
  20.8 2.0 %add_add_fusion = f32[8]{0:T(128)S(1)} fusion(f32[8]{0:T(128)} %param.12, f32[]{:T(128)} %bitcast.2, f32[]{:T(128)} %bitcast.1), kind=kLoop, calls=%fused_computation.18 | loop fusion | flops 16 | bytes 72 | tf_op jit(solution)/shard_map/add | solution.py:148
  22.8 0.1 broadcast_subtract_fusion
  22.9 0.6 fusion.4
  23.5 0.1 fusion.1
  23.5 1.3 %compare_select_fusion.1 = f32[128]{0:T(128)S(1)} fusion(pred[]{:T(512)S(6)} %lt.47, s32[]{:T(128)} %bitcast.4, f32[]{:T(128)S(6)} %convert_element_type.18, f32[]{:T(128)} %bitcast.3), kind=kLoop, calls=%fused_computation.11 | loop fusion | flops 896 | bytes 525 | tf_op jit(solution)/shard_map/jit(_where)/select_n | solution.py:173
  24.8 0.1 sub.31
  24.9 0.8 %broadcast_in_dim.40 = f32[64]{0:T(128)S(1)} reshape(f32[8,8]{1,0:T(8,128)} %param.11) | data formatting | bytes 512 | tf_op jit(solution)/shard_map/broadcast_in_dim | solution.py:160
  25.7 0.1 broadcast_in_dim.39.shift_ref
  25.8 0.8 %reciprocals.1.recip_ref = f32[64,128,128]{2,1,0:T(8,128)S(1)} custom-call(f32[64,128]{1,0:T(8,128)S(1)} %broadcast_in_dim.39.shift_ref, f32[128,128]{1,0:T(8,128)S(1)} %broadcast_add_fusion.sums_ref), custom_call_target="tpu_custom_call" | custom-call | tf_op jit(solution)/shard_map/reciprocals/pallas_call | solution.py:152
  26.6 0.1 broadcast_in_dim.41.amps_ref
  26.7 2.6 %energies.1 = f32[64,128]{1,0:T(8,128)S(1)} custom-call(bf16[8,8,128,128]{3,2,1,0:T(8,128)(2,1)S(1)} %copy-done.1, bf16[2,128,128]{2,1,0:T(8,128)(2,1)S(1)} %collective-permute-done.rows_ref, bf16[128,128]{1,0:T(8,128)(2,1)S(1)} %collective-permute-done.1.swap_ref, f32[64,128,128]{2,1,0:T(8,128)S(1)} %reciprocals.1.recip_ref, ...), custom_call_target="tpu_custom_call" | custom-call | tf_op jit(solution)/shard_map/energies/pallas_call | solution.py:176
  29.2 20.5 %all_to_all.22 = f32[64,1,128]{2,1,0:T(1,128)S(1)} all-to-all(f32[64,1,128]{2,1,0:T(1,128)S(1)} %bitcast.22), channel_id=1, replica_groups=mesh['yl'=4,'z'=8,'c'=2,'yh'=2,'x'=8] {'yh','yl','x'}, dimensions={0} | all-to-all | bytes 65536 | tf_op jit(solution)/shard_map/all_to_all | solution.py:185
  49.8 0.3 table.1
  50.1 23.4 %all_to_all.23 = f32[16,8,128]{2,1,0:T(8,128)S(1)} all-to-all(f32[16,8,128]{2,1,0:T(8,128)S(1)} %bitcast.21), channel_id=1, replica_groups=mesh['yl'=4,'z'=8,'c'=2,'yh'=2,'x'=8] {'z','c'}, dimensions={0} | all-to-all | bytes 131072 | tf_op jit(solution)/shard_map/all_to_all | solution.py:194
  73.4 0.7 lookup.1
  (7 shorter events, 0.0 us)
Async XLA Ops:
  0.6 0.9 %copy-start = (bf16[4,128,128]{2,1,0:T(8,128)(2,1)S(1)}, bf16[4,128,128]{2,1,0:T(8,128)(2,1)}, u32[]{:S(2)}) copy-start(bf16[4,128,128]{2,1,0:T(8,128)(2,1)} %param.10) | copy-start | bytes 393220
  0.6 26.0 %copy-start.1 = (bf16[8,8,128,128]{3,2,1,0:T(8,128)(2,1)S(1)}, bf16[8,8,128,128]{3,2,1,0:T(8,128)(2,1)}, u32[]{:S(2)}) copy-start(bf16[8,8,128,128]{3,2,1,0:T(8,128)(2,1)} %ints_ref.1) | copy-start | bytes 6291460
  2.4 24.2 %collective-permute-start = (bf16[2,128,128]{2,1,0:T(8,128)(2,1)S(1)}, bf16[2,128,128]{2,1,0:T(8,128)(2,1)S(1)}, u32[]{:S(2)}, u32[]{:S(2)}) collective-permute-start(bf16[2,128,128]{2,1,0:T(8,128)(2,1)S(1)} %pad_maximum_fusion), channel_id=1, source_target_pairs={{0,0},{1,1},{2,2},{3,3},{4,4},{5,5},{6,6},{7,7},{8,8},{9,9},{10,10... | collective-permute-start | bytes 196616 | tf_op jit(solution)/shard_map/ppermute | solution.py:142
  14.6 12.0 %collective-permute-start.1 = (bf16[128,128]{1,0:T(8,128)(2,1)S(1)}, bf16[128,128]{1,0:T(8,128)(2,1)S(1)}, u32[]{:S(2)}, u32[]{:S(2)}) collective-permute-start(bf16[128,128]{1,0:T(8,128)(2,1)S(1)} %get-tuple-element.16), channel_id=1, source_target_pairs={{0,0},{520,1},{2,2},{522,3},{4,4},{524,5},{6,6},{526,7},{513,8},{9... | collective-permute-start | bytes 98312 | tf_op jit(solution)/shard_map/ppermute | solution.py:143

commit v2 on v1

v2 whole, which is shorter than its diff:
```python
import jax
import jax.numpy as jnp
import numpy as np
from jax import lax
from jax.experimental import pallas as pl
from jax.experimental.pallas import tpu as pltpu
from jax.sharding import Mesh
from jax.sharding import PartitionSpec as P

AXES = ("yl", "z", "c", "yh", "x")
SIZES = (4, 8, 2, 2, 8)
GRP = ("yl", "z", "c")
BLK = ("yh", "x")
PLANE = ("yh", "yl", "x")
STACK = ("z", "c")
NO = 8
WORKERS = 4
SMALL = pltpu.CompilerParams(vmem_limit_bytes=12 * 1024 * 1024)
F32 = jnp.float32


def device_at(yl, z, c, yh, x):
    return ((((yl * 8) + z) * 2 + c) * 2 + yh) * 8 + x


def owners_of(yl, z, c, yh, x):
    low, high = z & 1, z >> 1 & 1
    none, one, more = yl == 0, yl == 1, yl > 1
    offset = none * (low + 2 * high + 4 * c) + one * (low + 4 * high + 8 * c) + more * (low + 2 * high + 8 * c)
    owner = (yh * 8 + x) ^ offset
    swapped = (owner & 1) << 3 | (owner & 6) ^ (yl << 1) | owner >> 3
    return owner, none * (owner ^ 9) + (1 - none) * swapped


def pair_at(owner, yl):
    return owner >> 1, (owner & 1) * 4 + ((owner >> 1 & 3) ^ yl)


def routes():
    first, second = [], []
    for yl, z, c, yh, x in np.ndindex(*SIZES):
        if z < WORKERS:
            here = device_at(yl, z, c, yh, x)
            for route, owner in zip((first, second), owners_of(yl, z, c, yh, x)):
                route.append((device_at(yl, z, c, owner >> 3, owner & 7), here))
    return first, second


def where_am_i():
    yl, z, c, yh, x = (lax.axis_index(axis) for axis in AXES)
    return yl, z, c, yh, x


def own_pairs():
    yl, z, c, yh, x = where_am_i()
    none = (yl == 0).astype(jnp.int32)
    one = (yl == 1).astype(jnp.int32)
    more = (yl > 1).astype(jnp.int32)
    low, high = z & 1, (z >> 1) & 1
    offset = none * (low + 2 * high + 4 * c) + one * (low + 4 * high + 8 * c) + more * (low + 2 * high + 8 * c)
    owner = (yh * 8 + x) ^ offset
    swapped = ((owner & 1) << 3) | ((owner & 6) ^ (yl << 1)) | (owner >> 3)
    other = none * (owner ^ 9) + (1 - none) * swapped
    return pair_at(owner, yl), pair_at(other, yl)


def rows_kernel(doubles_ref, coulomb_ref, out_ref, sems):
    yl, _, _, yh, x = where_am_i()
    row = (((yh * 8 + x) >> 1) & 3) ^ yl
    copies = [
        pltpu.make_async_copy(doubles_ref.at[row], out_ref.at[0], sems.at[0]),
        pltpu.make_async_copy(coulomb_ref.at[row], out_ref.at[1], sems.at[1]),
    ]
    for copy in copies:
        copy.start()
    for copy in copies:
        copy.wait()


def prep_kernel(ints_ref, trip_ref, count_ref, occ_ref, vir_ref, singles_ref, virs_ref,
                slab_ref, recip_ref, amps_ref, info_ref, first_ref, pair_ref, sem):
    occupied, width_block = singles_ref.shape
    width = virs_ref.shape[1]
    slots = first_ref.shape[0]
    _, z, _, yh, x = where_am_i()
    place = yh * 8 + x
    (j1, k1), (j2, k2) = own_pairs()
    diagonal = j1 == k1
    busy = z < WORKERS
    live = count_ref[0]
    slabs = pltpu.make_async_copy(ints_ref, slab_ref, sem)

    @pl.when(busy)
    def _():
        slabs.start()

    lane = lax.broadcasted_iota(jnp.int32, (1, 128), 1)
    mine = jnp.where(place < live, trip_ref[0, 0, place] + 16, -1)
    info = jnp.where(lane == mine, 1.0, 0.0)
    info = jnp.where(lane == 24, jnp.where(busy, j1 * NO + k1, -1).astype(F32), info)
    info = jnp.where(lane == 25, jnp.where(busy, j2 * NO + k2, -1).astype(F32), info)
    info = jnp.where(lane == 26, (trip_ref[1, 0, place] * NO + trip_ref[2, 0, place]).astype(F32), info)
    info_ref[...] = info

    sub = lax.broadcasted_iota(jnp.int32, (slots, 128), 0)
    lanes = lax.broadcasted_iota(jnp.int32, (slots, 128), 1)
    first_at = jnp.full((slots, 128), -1, jnp.int32)
    pair_at_ = jnp.full((slots, 128), -1, jnp.int32)
    for s in range(slots):
        first_at = jnp.where(sub == s, jnp.where(s < live, trip_ref[0, 0, s], -1), first_at)
        pair_at_ = jnp.where(sub == s, trip_ref[1, 0, s] * NO + trip_ref[2, 0, s], pair_at_)
    first_ref[...] = jnp.where(first_at == lanes, 1.0, 0.0)
    pair_ref[...] = jnp.where(pair_at_ == lanes, 1.0, 0.0)

    def fill(table, second, third, write_amps):
        across = jnp.broadcast_to(virs_ref[...], (width, width))
        sums = across.T + across

        def one_occ(i, carry):
            occ_sum = occ_ref[i] + occ_ref[second] + occ_ref[third]
            for a in range(width_block):
                r = i * width_block + a
                recip_ref[table, r] = 1.0 / ((occ_sum - vir_ref[place * width_block + a]) - sums)
                if write_amps:
                    amps_ref[pl.ds(r, 1), :] = jnp.full((1, 128), singles_ref[i, a], F32)
            return carry

        lax.fori_loop(0, occupied, one_occ, 0)

    @pl.when(busy)
    def _():
        fill(0, j1, k1, True)

    @pl.when(jnp.logical_and(busy, diagonal))
    def _():
        fill(1, j2, k2, False)

    @pl.when(busy)
    def _():
        slabs.wait()


def energy_kernel(ints_ref, one_ref, two_ref, recip_ref, amps_ref, info_ref, out_ref, sums_ref):
    occupied, width_block, width, _ = ints_ref.shape
    _, z, _, _, _ = where_am_i()
    (j1, k1), _ = own_pairs()
    diagonal = j1 == k1
    sums_ref[...] = jnp.zeros(sums_ref.shape, F32)

    def fold(value):
        return jnp.sum(value.reshape(width // 8, 8, width), axis=0)

    def both(couple):
        amps = jnp.concatenate([one_ref[0], two_ref[0]], axis=0)
        coupling_one = one_ref[1].astype(F32)
        coupling_two = two_ref[1].astype(F32)
        if couple:
            coupling_two = coupling_two.T

        def one_occ(i, carry):
            slab = ints_ref[i].reshape(width_block * width, width)
            products = lax.dot_general(slab, amps, (((1,), (1,)), ((), ())), preferred_element_type=F32)
            total_one = jnp.zeros((8, width), F32)
            total_two = jnp.zeros((8, width), F32)
            for a in range(width_block):
                r = i * width_block + a
                left = products[a * width:(a + 1) * width, :width]
                right = products[a * width:(a + 1) * width, width:]
                amp = amps_ref[pl.ds(r, 1), :]
                recip_one = recip_ref[0, r]
                if couple:
                    connected_one = right + left.T
                    connected_two = connected_one
                    recip_two = recip_one
                else:
                    connected_one = left + left.T
                    connected_two = right + right.T
                    recip_two = recip_ref[1, r]
                full_one = connected_one + amp * coupling_one
                full_two = connected_two + amp * coupling_two
                total_one = total_one + fold(full_one * full_one * recip_one)
                total_two = total_two + fold(full_two * full_two * recip_two)
            sums_ref[pl.ds(i, 1), :] = jnp.sum(total_one, axis=0, keepdims=True)
            sums_ref[pl.ds(i + occupied, 1), :] = jnp.sum(total_two, axis=0, keepdims=True)
            return carry

        lax.fori_loop(0, occupied, one_occ, 0)

    busy = z < WORKERS

    @pl.when(jnp.logical_and(busy, jnp.logical_not(diagonal)))
    def _():
        both(True)

    @pl.when(jnp.logical_and(busy, diagonal))
    def _():
        both(False)

    energies = jnp.sum(sums_ref[...], axis=1, keepdims=True)
    sub = lax.broadcasted_iota(jnp.int32, (2 * occupied, 128), 0)
    lane = lax.broadcasted_iota(jnp.int32, (2 * occupied, 128), 1)
    row = jnp.sum(jnp.where(sub == lane, energies, 0.0), axis=0, keepdims=True)
    out_ref[...] = jnp.broadcast_to(row + info_ref[...], out_ref.shape)


def table_kernel(in_ref, out_ref):
    got = in_ref[...]
    lane = lax.broadcasted_iota(jnp.int32, got.shape, 1)
    lane_at = lane.astype(F32)
    lists = got[:, 26:27] + 64.0

    def gathered(pick):
        return lax.dot_general(
            got,
            (pick == lane_at).astype(F32),
            (((0,), (0,)), ((), ())),
            precision=lax.Precision.HIGHEST,
            preferred_element_type=F32,
        )

    ones = gathered(jnp.where(lane < 64, got[:, 24:25], lists))
    twos = gathered(got[:, 25:26])
    low = lax.broadcasted_iota(jnp.int32, (8, 128), 1) < 64
    packed = jnp.where(low, ones[0:8] + twos[8:16], ones[16:24])
    peers = out_ref.shape[0] // 8
    out_ref[...] = jnp.broadcast_to(packed[None], (peers, 8, 128)).reshape(peers * 8, 128)


def final_kernel(in_ref, first_ref, pair_ref, trip_ref, mean_ref):
    peers = in_ref.shape[0] // 8
    table = jnp.sum(in_ref[...].reshape(peers, 8, 128), axis=0)
    counts = pltpu.roll(table, 64, 1)
    low = lax.broadcasted_iota(jnp.int32, (8, 128), 1) < 64
    weighted = jnp.where(low, table * counts, 0.0)
    mean_ref[...] = jnp.sum(jnp.sum(weighted, axis=0, keepdims=True), axis=1, keepdims=True) / 1024.0
    chosen = jnp.zeros((16, 128), F32)
    for i in range(8):
        chosen = chosen + first_ref[:, i:i + 1] * table[i:i + 1, :]
    values = jnp.sum(chosen * pair_ref[...], axis=1, keepdims=True)
    sub = lax.broadcasted_iota(jnp.int32, (16, 128), 0)
    lane = lax.broadcasted_iota(jnp.int32, (16, 128), 1)
    row = jnp.sum(jnp.where(sub == lane, values, 0.0), axis=0, keepdims=True)
    trip_ref[...] = row[:, :16]


def spaces(*kinds):
    return [pl.BlockSpec(memory_space=kind) for kind in kinds]


def vmem(count):
    return spaces(*[pltpu.VMEM] * count)


def kept(*arrays):
    return [pltpu.with_memory_space_constraint(a, pltpu.VMEM) for a in arrays]


def left_in_hbm(*arrays):
    return [pltpu.with_memory_space_constraint(a, pltpu.HBM) for a in arrays]


def rows_call(doubles, coulomb):
    _, width, depth = doubles.shape
    return pl.pallas_call(
        rows_kernel,
        out_shape=pltpu.VMEM((2, width, depth), doubles.dtype),
        in_specs=spaces(pl.ANY, pl.ANY),
        out_specs=vmem(1)[0],
        scratch_shapes=[pltpu.SemaphoreType.DMA((2,))],
        compiler_params=SMALL,
        name="rows",
    )(*left_in_hbm(doubles, coulomb))


def prep_call(integrals, lists, tile_count, occ_energy, vir_energy, singles):
    occupied, width_block = singles.shape
    width = vir_energy.shape[0]
    slots = lists.shape[2]
    return pl.pallas_call(
        prep_kernel,
        out_shape=(
            pltpu.VMEM(integrals.shape, integrals.dtype),
            pltpu.VMEM((2, occupied * width_block, width, width), F32),
            pltpu.VMEM((occupied * width_block, width), F32),
            pltpu.VMEM((1, 128), F32),
            pltpu.VMEM((slots, 128), F32),
            pltpu.VMEM((slots, 128), F32),
        ),
        in_specs=spaces(pl.ANY, *[pltpu.SMEM] * 5, pltpu.VMEM),
        out_specs=tuple(vmem(6)),
        scratch_shapes=[pltpu.SemaphoreType.DMA],
        compiler_params=SMALL,
        name="prep",
    )(*left_in_hbm(integrals, lists), tile_count, *left_in_hbm(occ_energy, vir_energy, singles, vir_energy[None]))


def energy_call(slabs, one, two, recip, amps, info):
    occupied, _, width, _ = slabs.shape
    return pl.pallas_call(
        energy_kernel,
        out_shape=pltpu.VMEM((64, 128), F32),
        in_specs=vmem(6),
        out_specs=vmem(1)[0],
        scratch_shapes=[pltpu.VMEM((2 * occupied, width), F32)],
        compiler_params=SMALL,
        name="energies",
    )(*kept(slabs, one, two, recip, amps, info))


def table_call(message):
    return pl.pallas_call(
        table_kernel,
        out_shape=pltpu.VMEM((128, 128), F32),
        in_specs=vmem(1),
        out_specs=vmem(1)[0],
        compiler_params=SMALL,
        name="table",
    )(*kept(message))


def final_call(tables, first_hot, pair_hot):
    slots = first_hot.shape[0]
    return pl.pallas_call(
        final_kernel,
        out_shape=(jax.ShapeDtypeStruct((1, slots), F32), jax.ShapeDtypeStruct((1, 1), F32)),
        in_specs=vmem(3),
        out_specs=tuple(vmem(2)),
        compiler_params=SMALL,
        name="lookup",
    )(*kept(tables, first_hot, pair_hot))


def body(integrals, doubles, coulomb, singles, occ_energy, vir_energy, triplets, tile_count):
    first, second = routes()
    sent = rows_call(doubles, coulomb)
    one = lax.ppermute(sent, AXES, first)
    two = lax.ppermute(sent, AXES, second)
    lists = jnp.transpose(triplets, (2, 0, 1))
    slabs, recip, amps, info, first_hot, pair_hot = prep_call(integrals, lists, tile_count, occ_energy, vir_energy, singles)
    message = energy_call(slabs, one, two, recip, amps, info)
    message = lax.all_to_all(message, PLANE, 0, 0, tiled=True)
    tables = table_call(message)
    tables = lax.all_to_all(tables, STACK, 0, 0, tiled=True)
    trip, mean = final_call(tables, first_hot, pair_hot)
    return trip, mean.reshape(())


def solution(mesh):
    fine = Mesh(mesh.devices.reshape(SIZES), AXES)
    in_specs = (
        P(None, BLK, None, None),
        P(BLK, None, None),
        P(BLK, None, None),
        P(None, BLK),
        P(),
        P(),
        P(GRP, None, None),
        P(GRP),
    )
    out_specs = (P(GRP, None), P())
    return jax.shard_map(body, mesh=fine, in_specs=in_specs, out_specs=out_specs, check_vma=False)
```

time: 74.5 us -> 65.9 us (0.88)
  blocking collectives: 43.9 us -> 37.1 us
  other arithmetic: 5.5 us -> 0 us
  local copies, waits for them, and re-layouts: 4.75 us -> 0 us
  Pallas kernels: 4.37 us -> 8.5 us
  waiting for transfers between devices: 0.01 us -> 2.88 us
  starting transfers between devices: 14.2 us -> 15.8 us
    all_to_all x1, blocking collectives: 20.5 us -> 16.1 us  [body(): message = lax.all_to_all(message, PLANE, 0, 0, tiled=True)]
    pallas_call x4 -> x5, Pallas kernels: 4.37 us -> 8.5 us  [the longest x1 4.25 us: energy_call(): pl.pallas_call(energy_kernel, out_shape=pltpu.VMEM((64, 128), F32), in_sp...]
    add x3 -> x0, other arithmetic: 3.35 us -> none  [the longest x1 1.95 us: body(): occ_sums = occ_energy + occ_energy[second] + occ_energy[third]]
    ppermute x2, waiting for transfers between devices: 0.01 us -> 2.88 us  [the longest x1 2.87 us: body(): one = lax.ppermute(sent, AXES, first)]
    all_to_all x1, blocking collectives: 23.4 us -> 21 us  [body(): tables = lax.all_to_all(tables, STACK, 0, 0, tiled=True)]
    dynamic_slice x3 -> x0, local copies, waits for them, and re-layouts: 2.06 us -> none  [the longest x1 1.32 us: body(): occ_sums = occ_energy + occ_energy[second] + occ_energy[third]]
    ppermute x2, starting transfers between devices: 14.2 us -> 15.8 us  [the longest x1 12.8 us: body(): two = lax.ppermute(sent, AXES, second)]
    select_n x1 -> x0, other arithmetic: 1.3 us -> none  [body(): info = jnp.where(lane == 17, my_pair.astype(jnp.float32), info)]
  transfers between devices with their start and end apart: 2 -> 2, of which waited for: 0 -> 1; matrix products, arithmetic and copies ran while one was open for 12% -> 0% of each run, Pallas kernels for 1% -> 4%
where the time goes in v2:
time: 65.9 us; the launch traced here: 65.5 us
  blocking collectives  37.1 us (56%)
  starting transfers between devices  15.8 us (24%)
  Pallas kernels  8.5 us (13%)
  waiting for transfers between devices  2.88 us (4%)
  between operations  1.33 us (2%)
    all_to_all x1, blocking collectives, body(): tables = lax.all_to_all(tables, STACK, 0, 0, tiled=True)  21 us
    all_to_all x1, blocking collectives, body(): message = lax.all_to_all(message, PLANE, 0, 0, tiled=True)  16.1 us
    ppermute x1, starting transfers between devices, body(): two = lax.ppermute(sent, AXES, second)  12.8 us
    pallas_call x1, Pallas kernels, energy_call(): pl.pallas_call(energy_kernel, out_shape=pltpu.VMEM((64, 128), F32), in_sp...  4.25 us
    ppermute x1, starting transfers between devices, body(): one = lax.ppermute(sent, AXES, first)  2.98 us
    ppermute x1, waiting for transfers between devices, body(): one = lax.ppermute(sent, AXES, first)  2.87 us
    pallas_call x1, Pallas kernels, prep_call(): pl.pallas_call(prep_kernel, out_shape=(pltpu.VMEM(integrals.shape, integr...  2.39 us
  transfers between devices with their start and end apart: 2, of which 1 were waited for; matrix products, arithmetic and copies ran while one was open for 0% of the time, Pallas kernels for 4%

profile of v2, /device:TPU:1, one launch (start us, length us, event | category | flops | bytes accessed | tf_op | source)
XLA Modules:
  0.0 65.5 jit_solution(5694385539435910357)
XLA Ops:
  0.6 0.8 %rows.1 = bf16[2,128,128]{2,1,0:T(8,128)(2,1)S(1)} custom-call(bf16[4,128,128]{2,1,0:T(8,128)(2,1)} %doubles_ref.1, bf16[4,128,128]{2,1,0:T(8,128)(2,1)} %coulomb_ref.1), custom_call_target="tpu_custom_call" | custom-call | tf_op jit(solution)/shard_map/rows/pallas_call | solution.py:264
  1.4 12.8 %collective-permute-start.1 = (bf16[2,128,128]{2,1,0:T(8,128)(2,1)S(1)}, bf16[2,128,128]{2,1,0:T(8,128)(2,1)S(1)}, u32[]{:S(2)}, u32[]{:S(2)}) collective-permute-start(bf16[2,128,128]{2,1,0:T(8,128)(2,1)S(1)} %rows.1), channel_id=1, source_target_pairs={{9,0},{8,1},{11,2},{10,3},{13,4},{12,5},{15,6},{14,7},{1,8},{0,9},... | collective-permute-start | bytes 196616 | tf_op jit(solution)/shard_map/ppermute | solution.py:337
  14.2 3.0 %collective-permute-start = (bf16[2,128,128]{2,1,0:T(8,128)(2,1)S(1)}, bf16[2,128,128]{2,1,0:T(8,128)(2,1)S(1)}, u32[]{:S(2)}, u32[]{:S(2)}) collective-permute-start(bf16[2,128,128]{2,1,0:T(8,128)(2,1)S(1)} %rows.1), channel_id=1, source_target_pairs={{0,0},{1,1},{2,2},{3,3},{4,4},{5,5},{6,6},{7,7},{8,8},{9,9},{10,10... | collective-permute-start | bytes 196616 | tf_op jit(solution)/shard_map/ppermute | solution.py:336
  17.9 2.4 %prep.1 = (bf16[8,8,128,128]{3,2,1,0:T(8,128)(2,1)S(1)}, f32[2,64,128,128]{3,2,1,0:T(8,128)S(1)}, f32[64,128]{1,0:T(8,128)S(1)}, f32[1,128]{1,0:T(1,128)S(1)}, f...) custom-call(bf16[8,8,128,128]{3,2,1,0:T(8,128)(2,1)} %ints_ref.1, s32[3,1,16]{2,1,0:T(1,128)} %bitcast.14, ...), custom_call_target="tpu_custom_call" | custom-call | tf_op jit(solution)/shard_map/prep/pallas_call | solution.py:279
  20.3 0.0 collective-permute-done.1.two_ref
  20.3 2.9 %collective-permute-done.one_ref = bf16[2,128,128]{2,1,0:T(8,128)(2,1)S(1)} collective-permute-done((bf16[2,128,128]{2,1,0:T(8,128)(2,1)S(1)}, bf16[2,128,128]{2,1,0:T(8,128)(2,1)S(1)}, u32[]{:S(2)}, u32[]{:S(2)}) %collective-permute-start) | collective-permute-done | bytes 65568 | tf_op jit(solution)/shard_map/ppermute | solution.py:336
  23.1 4.2 %energies.1 = f32[64,128]{1,0:T(8,128)S(1)} custom-call(bf16[8,8,128,128]{3,2,1,0:T(8,128)(2,1)S(1)} %get-tuple-element.10.ints_ref, bf16[2,128,128]{2,1,0:T(8,128)(2,1)S(1)} %collective-permute-done.one_ref, bf16[2,128,128]{2,1,0:T(8,128)(2,1)S(1)} %collective-permute-done.1.two_ref, f32[2,64,128,128]{3,2,1,0:T(8,128)S(1)} %get-tuple-element.11.recip_ref, ...), custom_call_target="tpu_custom_call" | custom-call | tf_op jit(solution)/shard_map/energies/pallas_call | solution.py:299
  27.4 16.1 %all_to_all.22 = f32[64,1,128]{2,1,0:T(1,128)S(1)} all-to-all(f32[64,1,128]{2,1,0:T(1,128)S(1)} %bitcast.11), channel_id=1, replica_groups=mesh['yl'=4,'z'=8,'c'=2,'yh'=2,'x'=8] {'yh','yl','x'}, dimensions={0} | all-to-all | bytes 65536 | tf_op jit(solution)/shard_map/all_to_all | solution.py:341
  43.5 0.4 table.1
  43.8 21.0 %all_to_all.23 = f32[16,8,128]{2,1,0:T(8,128)S(1)} all-to-all(f32[16,8,128]{2,1,0:T(8,128)S(1)} %bitcast.10), channel_id=1, replica_groups=mesh['yl'=4,'z'=8,'c'=2,'yh'=2,'x'=8] {'z','c'}, dimensions={0} | all-to-all | bytes 131072 | tf_op jit(solution)/shard_map/all_to_all | solution.py:343
  64.8 0.7 %lookup.1 = (f32[1,16]{1,0:T(1,128)}, f32[1,1]{1,0:T(1,128)}) custom-call(f32[128,128]{1,0:T(8,128)S(1)} %bitcast.9, f32[16,128]{1,0:T(8,128)S(1)} %get-tuple-element.14.first_ref, f32[16,128]{1,0:T(8,128)S(1)} %get-tuple-element.15.pair_ref), custom_call_target="tpu_custom_call" | custom-call | tf_op jit(solution)/shard_map/lookup/pallas_call | solution.py:323
Async XLA Ops:
  1.4 18.8 %collective-permute-start.1 = (bf16[2,128,128]{2,1,0:T(8,128)(2,1)S(1)}, bf16[2,128,128]{2,1,0:T(8,128)(2,1)S(1)}, u32[]{:S(2)}, u32[]{:S(2)}) collective-permute-start(bf16[2,128,128]{2,1,0:T(8,128)(2,1)S(1)} %rows.1), channel_id=1, source_target_pairs={{9,0},{8,1},{11,2},{10,3},{13,4},{12,5},{15,6},{14,7},{1,8},{0,9},... | collective-permute-start | bytes 196616 | tf_op jit(solution)/shard_map/ppermute | solution.py:337
  14.2 8.9 %collective-permute-start = (bf16[2,128,128]{2,1,0:T(8,128)(2,1)S(1)}, bf16[2,128,128]{2,1,0:T(8,128)(2,1)S(1)}, u32[]{:S(2)}, u32[]{:S(2)}) collective-permute-start(bf16[2,128,128]{2,1,0:T(8,128)(2,1)S(1)} %rows.1), channel_id=1, source_target_pairs={{0,0},{1,1},{2,2},{3,3},{4,4},{5,5},{6,6},{7,7},{8,8},{9,9},{10,10... | collective-permute-start | bytes 196616 | tf_op jit(solution)/shard_map/ppermute | solution.py:336

commit v3 on v2

--- a/solution.py
+++ b/solution.py
@@ -23,17 +23,16 @@
     return ((((yl * 8) + z) * 2 + c) * 2 + yh) * 8 + x
 
 
-def owners_of(yl, z, c, yh, x):
-    low, high = z & 1, z >> 1 & 1
-    none, one, more = yl == 0, yl == 1, yl > 1
-    offset = none * (low + 2 * high + 4 * c) + one * (low + 4 * high + 8 * c) + more * (low + 2 * high + 8 * c)
-    owner = (yh * 8 + x) ^ offset
-    swapped = (owner & 1) << 3 | (owner & 6) ^ (yl << 1) | owner >> 3
+def owners_of(yl, z, c, yh, x, none, one):
+    low, high = z & 1, (z >> 1) & 1
+    offset = none * (2 * low + 4 * high) + one * (low + 4 * high) + (1 - none - one) * (low + 2 * high)
+    owner = (yh * 8 + x) ^ (offset + 8 * c)
+    swapped = ((owner & 1) << 3) | ((owner & 6) ^ (yl << 1)) | (owner >> 3)
     return owner, none * (owner ^ 9) + (1 - none) * swapped
 
 
 def pair_at(owner, yl):
-    return owner >> 1, (owner & 1) * 4 + ((owner >> 1 & 3) ^ yl)
+    return owner >> 1, (owner & 1) * 4 + (((owner >> 1) & 3) ^ yl)
 
 
 def routes():
@@ -41,8 +40,10 @@
     for yl, z, c, yh, x in np.ndindex(*SIZES):
         if z < WORKERS:
             here = device_at(yl, z, c, yh, x)
-            for route, owner in zip((first, second), owners_of(yl, z, c, yh, x)):
-                route.append((device_at(yl, z, c, owner >> 3, owner & 7), here))
+            owner, other = owners_of(yl, z, c, yh, x, int(yl == 0), int(yl == 1))
+            crosses = int(other >> 3 != yh) if yl & 1 else 1
+            first.append((device_at(yl ^ (2 * c), z, c, owner >> 3, owner & 7), here))
+            second.append((device_at(yl ^ (2 * crosses), z, c, other >> 3, other & 7), here))
     return first, second
 
 
@@ -53,23 +54,25 @@
 
 def own_pairs():
     yl, z, c, yh, x = where_am_i()
-    none = (yl == 0).astype(jnp.int32)
-    one = (yl == 1).astype(jnp.int32)
-    more = (yl > 1).astype(jnp.int32)
-    low, high = z & 1, (z >> 1) & 1
-    offset = none * (low + 2 * high + 4 * c) + one * (low + 4 * high + 8 * c) + more * (low + 2 * high + 8 * c)
-    owner = (yh * 8 + x) ^ offset
-    swapped = ((owner & 1) << 3) | ((owner & 6) ^ (yl << 1)) | (owner >> 3)
-    other = none * (owner ^ 9) + (1 - none) * swapped
+    none, one = (yl == 0).astype(jnp.int32), (yl == 1).astype(jnp.int32)
+    owner, other = owners_of(yl, z, c, yh, x, none, one)
     return pair_at(owner, yl), pair_at(other, yl)
 
 
-def rows_kernel(doubles_ref, coulomb_ref, out_ref, sems):
-    yl, _, _, yh, x = where_am_i()
-    row = (((yh * 8 + x) >> 1) & 3) ^ yl
+def sent_rows(yl, c, yh, x):
+    low_bits = ((yh * 8 + x) >> 1) & 3
+    crosses = (1 - (yl & 1)) | (yh ^ (x & 1) ^ c)
+    return low_bits ^ yl ^ (2 * c), low_bits ^ yl ^ (2 * crosses)
+
+
+def rows_kernel(doubles_ref, coulomb_ref, first_ref, second_ref, sems):
+    yl, _, c, yh, x = where_am_i()
+    first, second = sent_rows(yl, c, yh, x)
     copies = [
-        pltpu.make_async_copy(doubles_ref.at[row], out_ref.at[0], sems.at[0]),
-        pltpu.make_async_copy(coulomb_ref.at[row], out_ref.at[1], sems.at[1]),
+        pltpu.make_async_copy(doubles_ref.at[first], first_ref.at[0], sems.at[0]),
+        pltpu.make_async_copy(coulomb_ref.at[first], first_ref.at[1], sems.at[1]),
+        pltpu.make_async_copy(doubles_ref.at[second], second_ref.at[0], sems.at[2]),
+        pltpu.make_async_copy(coulomb_ref.at[second], second_ref.at[1], sems.at[3]),
     ]
     for copy in copies:
         copy.start()
@@ -184,7 +187,7 @@
             sums_ref[pl.ds(i + occupied, 1), :] = jnp.sum(total_two, axis=0, keepdims=True)
             return carry
 
-        lax.fori_loop(0, occupied, one_occ, 0)
+        lax.fori_loop(0, occupied, one_occ, 0, unroll=True)
 
     busy = z < WORKERS
 
@@ -263,10 +266,10 @@
     _, width, depth = doubles.shape
     return pl.pallas_call(
         rows_kernel,
-        out_shape=pltpu.VMEM((2, width, depth), doubles.dtype),
+        out_shape=(pltpu.VMEM((2, width, depth), doubles.dtype),) * 2,
         in_specs=spaces(pl.ANY, pl.ANY),
-        out_specs=vmem(1)[0],
-        scratch_shapes=[pltpu.SemaphoreType.DMA((2,))],
+        out_specs=tuple(vmem(2)),
+        scratch_shapes=[pltpu.SemaphoreType.DMA((4,))],
         compiler_params=SMALL,
         name="rows",
     )(*left_in_hbm(doubles, coulomb))
@@ -332,9 +335,9 @@
 
 def body(integrals, doubles, coulomb, singles, occ_energy, vir_energy, triplets, tile_count):
     first, second = routes()
-    sent = rows_call(doubles, coulomb)
-    one = lax.ppermute(sent, AXES, first)
-    two = lax.ppermute(sent, AXES, second)
+    sent_first, sent_second = rows_call(doubles, coulomb)
+    one = lax.ppermute(sent_first, AXES, first)
+    two = lax.ppermute(sent_second, AXES, second)
     lists = jnp.transpose(triplets, (2, 0, 1))
     slabs, recip, amps, info, first_hot, pair_hot = prep_call(integrals, lists, tile_count, occ_energy, vir_energy, singles)
     message = energy_call(slabs, one, two, recip, amps, info)

time: 65.9 us -> 64.5 us (0.979)
  blocking collectives: 37.1 us -> 42.2 us
  waiting for transfers between devices: 2.88 us -> 0.01 us
  Pallas kernels: 8.5 us -> 6.32 us
  starting transfers between devices: 15.8 us -> 14.2 us
    all_to_all x1, blocking collectives: 16.1 us -> 21.1 us  [body(): message = lax.all_to_all(message, PLANE, 0, 0, tiled=True)]
    ppermute x2, waiting for transfers between devices: 2.88 us -> 0.01 us  [the longest x1 0.01 us: body(): one = lax.ppermute(sent_first, AXES, first)]
    pallas_call x1, Pallas kernels: 4.25 us -> 2 us  [energy_call(): pl.pallas_call(energy_kernel, out_shape=pltpu.VMEM((64, 128), F32), in_sp...]
    ppermute x2, starting transfers between devices: 15.8 us -> 14.2 us  [the longest x1 7.38 us: body(): one = lax.ppermute(sent_first, AXES, first)]
  transfers between devices with their start and end apart: 2 -> 2, of which waited for: 1 -> 0; matrix products, arithmetic and copies ran while one was open for 0% -> 0% of each run, Pallas kernels for 4% -> 4%
where the time goes in v3:
time: 64.5 us; the launch traced here: 64.1 us
  blocking collectives  42.2 us (65%)
  starting transfers between devices  14.2 us (22%)
  Pallas kernels  6.32 us (10%)
  between operations  1.33 us (2%)
    all_to_all x1, blocking collectives, body(): message = lax.all_to_all(message, PLANE, 0, 0, tiled=True)  21.1 us
    all_to_all x1, blocking collectives, body(): tables = lax.all_to_all(tables, STACK, 0, 0, tiled=True)  21.1 us
    ppermute x1, starting transfers between devices, body(): one = lax.ppermute(sent_first, AXES, first)  7.38 us
    ppermute x1, starting transfers between devices, body(): two = lax.ppermute(sent_second, AXES, second)  6.84 us
    pallas_call x1, Pallas kernels, prep_call(): pl.pallas_call(prep_kernel, out_shape=(pltpu.VMEM(integrals.shape, integr...  2.39 us
    pallas_call x1, Pallas kernels, energy_call(): pl.pallas_call(energy_kernel, out_shape=pltpu.VMEM((64, 128), F32), in_sp...  2 us
  transfers between devices with their start and end apart: 2, of which 0 were waited for; matrix products, arithmetic and copies ran while one was open for 0% of the time, Pallas kernels for 4%

profile of v3, /device:TPU:1, one launch (start us, length us, event | category | flops | bytes accessed | tf_op | source)
XLA Modules:
  0.0 64.1 jit_solution(6557544622869433743)
XLA Ops:
  0.6 0.9 %rows.1 = (bf16[2,128,128]{2,1,0:T(8,128)(2,1)S(1)}, bf16[2,128,128]{2,1,0:T(8,128)(2,1)S(1)}) custom-call(bf16[4,128,128]{2,1,0:T(8,128)(2,1)} %doubles_ref.1, bf16[4,128,128]{2,1,0:T(8,128)(2,1)} %coulomb_ref.1), custom_call_target="tpu_custom_call" | custom-call | tf_op jit(solution)/shard_map/rows/pallas_call | solution.py:267
  1.5 7.4 %collective-permute-start = (bf16[2,128,128]{2,1,0:T(8,128)(2,1)S(1)}, bf16[2,128,128]{2,1,0:T(8,128)(2,1)S(1)}, u32[]{:S(2)}, u32[]{:S(2)}) collective-permute-start(bf16[2,128,128]{2,1,0:T(8,128)(2,1)S(1)} %get-tuple-element.13), channel_id=1, source_target_pairs={{0,0},{1,1},{2,2},{3,3},{4,4},{5,5},{6,6},{7,7},{8,8},{9,9},{10,10... | collective-permute-start | bytes 196616 | tf_op jit(solution)/shard_map/ppermute | solution.py:339
  8.9 6.8 %collective-permute-start.1 = (bf16[2,128,128]{2,1,0:T(8,128)(2,1)S(1)}, bf16[2,128,128]{2,1,0:T(8,128)(2,1)S(1)}, u32[]{:S(2)}, u32[]{:S(2)}) collective-permute-start(bf16[2,128,128]{2,1,0:T(8,128)(2,1)S(1)} %get-tuple-element.14), channel_id=1, source_target_pairs={{521,0},{520,1},{523,2},{522,3},{525,4},{524,5},{527,6},{526,7},{5... | collective-permute-start | bytes 196616 | tf_op jit(solution)/shard_map/ppermute | solution.py:340
  16.4 2.4 %prep.1 = (bf16[8,8,128,128]{3,2,1,0:T(8,128)(2,1)S(1)}, f32[2,64,128,128]{3,2,1,0:T(8,128)S(1)}, f32[64,128]{1,0:T(8,128)S(1)}, f32[1,128]{1,0:T(1,128)S(1)}, f...) custom-call(bf16[8,8,128,128]{3,2,1,0:T(8,128)(2,1)} %ints_ref.1, s32[3,1,16]{2,1,0:T(1,128)} %bitcast.14, ...), custom_call_target="tpu_custom_call" | custom-call | tf_op jit(solution)/shard_map/prep/pallas_call | solution.py:282
  18.8 0.0 collective-permute-done.one_ref
  18.8 0.0 collective-permute-done.1.two_ref
  18.8 2.0 %energies.1 = f32[64,128]{1,0:T(8,128)S(1)} custom-call(bf16[8,8,128,128]{3,2,1,0:T(8,128)(2,1)S(1)} %get-tuple-element.12.ints_ref, bf16[2,128,128]{2,1,0:T(8,128)(2,1)S(1)} %collective-permute-done.one_ref, bf16[2,128,128]{2,1,0:T(8,128)(2,1)S(1)} %collective-permute-done.1.two_ref, f32[2,64,128,128]{3,2,1,0:T(8,128)S(1)} %get-tuple-element.15.recip_ref, ...), custom_call_target="tpu_custom_call" | custom-call | tf_op jit(solution)/shard_map/energies/pallas_call | solution.py:302
  20.8 21.1 %all_to_all.22 = f32[64,1,128]{2,1,0:T(1,128)S(1)} all-to-all(f32[64,1,128]{2,1,0:T(1,128)S(1)} %bitcast.11), channel_id=1, replica_groups=mesh['yl'=4,'z'=8,'c'=2,'yh'=2,'x'=8] {'yh','yl','x'}, dimensions={0} | all-to-all | bytes 65536 | tf_op jit(solution)/shard_map/all_to_all | solution.py:344
  41.9 0.4 table.1
  42.3 21.1 %all_to_all.23 = f32[16,8,128]{2,1,0:T(8,128)S(1)} all-to-all(f32[16,8,128]{2,1,0:T(8,128)S(1)} %bitcast.10), channel_id=1, replica_groups=mesh['yl'=4,'z'=8,'c'=2,'yh'=2,'x'=8] {'z','c'}, dimensions={0} | all-to-all | bytes 131072 | tf_op jit(solution)/shard_map/all_to_all | solution.py:346
  63.4 0.7 %lookup.1 = (f32[1,16]{1,0:T(1,128)}, f32[1,1]{1,0:T(1,128)}) custom-call(f32[128,128]{1,0:T(8,128)S(1)} %bitcast.9, f32[16,128]{1,0:T(8,128)S(1)} %get-tuple-element.18.first_ref, f32[16,128]{1,0:T(8,128)S(1)} %get-tuple-element.19.pair_ref), custom_call_target="tpu_custom_call" | custom-call | tf_op jit(solution)/shard_map/lookup/pallas_call | solution.py:326
Async XLA Ops:
  1.5 17.3 %collective-permute-start = (bf16[2,128,128]{2,1,0:T(8,128)(2,1)S(1)}, bf16[2,128,128]{2,1,0:T(8,128)(2,1)S(1)}, u32[]{:S(2)}, u32[]{:S(2)}) collective-permute-start(bf16[2,128,128]{2,1,0:T(8,128)(2,1)S(1)} %get-tuple-element.13), channel_id=1, source_target_pairs={{0,0},{1,1},{2,2},{3,3},{4,4},{5,5},{6,6},{7,7},{8,8},{9,9},{10,10... | collective-permute-start | bytes 196616 | tf_op jit(solution)/shard_map/ppermute | solution.py:339
  8.9 9.9 %collective-permute-start.1 = (bf16[2,128,128]{2,1,0:T(8,128)(2,1)S(1)}, bf16[2,128,128]{2,1,0:T(8,128)(2,1)S(1)}, u32[]{:S(2)}, u32[]{:S(2)}) collective-permute-start(bf16[2,128,128]{2,1,0:T(8,128)(2,1)S(1)} %get-tuple-element.14), channel_id=1, source_target_pairs={{521,0},{520,1},{523,2},{522,3},{525,4},{524,5},{527,6},{526,7},{5... | collective-permute-start | bytes 196616 | tf_op jit(solution)/shard_map/ppermute | solution.py:340

commit v4 on v2

--- a/solution.py
+++ b/solution.py
@@ -23,27 +23,49 @@
     return ((((yl * 8) + z) * 2 + c) * 2 + yh) * 8 + x
 
 
-def owners_of(yl, z, c, yh, x):
-    low, high = z & 1, z >> 1 & 1
-    none, one, more = yl == 0, yl == 1, yl > 1
-    offset = none * (low + 2 * high + 4 * c) + one * (low + 4 * high + 8 * c) + more * (low + 2 * high + 8 * c)
-    owner = (yh * 8 + x) ^ offset
-    swapped = (owner & 1) << 3 | (owner & 6) ^ (yl << 1) | owner >> 3
-    return owner, none * (owner ^ 9) + (1 - none) * swapped
-
-
-def pair_at(owner, yl):
-    return owner >> 1, (owner & 1) * 4 + ((owner >> 1 & 3) ^ yl)
+OWNERS = (
+    (0x62d73195cf4eb80a, 0x573db2f106a48ec9, 0xf1b45763a92cd0e8, 0x3f71d5096c824abe,
+     0x19532b76facde480, 0x731b465fe0982dac, 0x05421d3798ebacf6, 0x942573108edacb6f),
+    (0x51fd36780ebc24a9, 0x92514dbf78e3ac60, 0xf315c709e42ab8d6, 0x6f43d51792cbe08a,
+     0x76325bf1894dca0e, 0x1974b0356a82decf, 0x859c2160afd43be7, 0x072b1356fcae4d98),
+    (0x38b9d6f12e0a547c, 0x709a4b15f8326cde, 0xf13b6709ea2d45c8, 0x0b253ce71f98ad46,
+     0x1952b37fa084ce6d, 0x924375de01acb68f, 0x83145d6092cbeaf7, 0x27a1c45689b3dfe0),
+    (0xb39746e5d2108fca, 0x3a2b9d71c80e654f, 0x710965d3ac28bef4, 0x5b731f4d20a9c8e6,
+     0x12a0d3f79b84e65c, 0x09327e5f81cba46d, 0x27b154360a9cfd8e, 0xf0153762e9ba4cd8),
+)
+APART = 2
+
+
+def owner_table():
+    digits = [[[int(d, 16) for d in f"{code:016x}"] for code in codes] for codes in OWNERS]
+    return np.array(digits, np.int32).reshape(-1)
+
+
+def owner_index(yl, z, c, yh, x):
+    return (((yl ^ (2 * yh)) * WORKERS + z % WORKERS) * 2 + c) * 16 + yh * 8 + x
+
+
+def pairs_of(owner, u, where):
+    swapped = ((owner & 1) << 3) | ((owner & 6) ^ (u << 1)) | (owner >> 3)
+    other = where(swapped == owner, owner ^ APART, swapped)
+    return other, pair_at(owner, u), pair_at(other, u)
+
+
+def pair_at(owner, u):
+    return owner >> 1, (owner & 1) * 4 + (((owner >> 1) & 3) ^ u)
 
 
 def routes():
-    first, second = [], []
+    table, near, far = owner_table(), [], []
     for yl, z, c, yh, x in np.ndindex(*SIZES):
         if z < WORKERS:
-            here = device_at(yl, z, c, yh, x)
-            for route, owner in zip((first, second), owners_of(yl, z, c, yh, x)):
-                route.append((device_at(yl, z, c, owner >> 3, owner & 7), here))
-    return first, second
+            here, u = device_at(yl, z, c, yh, x), yl ^ (2 * yh)
+            owner = int(table[owner_index(yl, z, c, yh, x)])
+            other, _, _ = pairs_of(owner, u, lambda a, b, c: b if a else c)
+            for route, block in ((near, owner), (far, other)):
+                half = block >> 3
+                route.append((device_at(u ^ (2 * half), z, c, half, block & 7), here))
+    return near, far
 
 
 def where_am_i():
@@ -51,22 +73,9 @@
     return yl, z, c, yh, x
 
 
-def own_pairs():
-    yl, z, c, yh, x = where_am_i()
-    none = (yl == 0).astype(jnp.int32)
-    one = (yl == 1).astype(jnp.int32)
-    more = (yl > 1).astype(jnp.int32)
-    low, high = z & 1, (z >> 1) & 1
-    offset = none * (low + 2 * high + 4 * c) + one * (low + 4 * high + 8 * c) + more * (low + 2 * high + 8 * c)
-    owner = (yh * 8 + x) ^ offset
-    swapped = ((owner & 1) << 3) | ((owner & 6) ^ (yl << 1)) | (owner >> 3)
-    other = none * (owner ^ 9) + (1 - none) * swapped
-    return pair_at(owner, yl), pair_at(other, yl)
-
-
 def rows_kernel(doubles_ref, coulomb_ref, out_ref, sems):
     yl, _, _, yh, x = where_am_i()
-    row = (((yh * 8 + x) >> 1) & 3) ^ yl
+    row = (((yh * 8 + x) >> 1) & 3) ^ yl ^ (2 * yh)
     copies = [
         pltpu.make_async_copy(doubles_ref.at[row], out_ref.at[0], sems.at[0]),
         pltpu.make_async_copy(coulomb_ref.at[row], out_ref.at[1], sems.at[1]),
@@ -77,14 +86,15 @@
         copy.wait()
 
 
-def prep_kernel(ints_ref, trip_ref, count_ref, occ_ref, vir_ref, singles_ref, virs_ref,
+def prep_kernel(ints_ref, owners_ref, trip_ref, count_ref, occ_ref, vir_ref, singles_ref, virs_ref,
                 slab_ref, recip_ref, amps_ref, info_ref, first_ref, pair_ref, sem):
     occupied, width_block = singles_ref.shape
     width = virs_ref.shape[1]
     slots = first_ref.shape[0]
-    _, z, _, yh, x = where_am_i()
+    yl, z, c, yh, x = where_am_i()
     place = yh * 8 + x
-    (j1, k1), (j2, k2) = own_pairs()
+    owner = owners_ref[owner_index(yl, z, c, yh, x)]
+    _, (j1, k1), (j2, k2) = pairs_of(owner, yl ^ (2 * yh), jnp.where)
     diagonal = j1 == k1
     busy = z < WORKERS
     live = count_ref[0]
@@ -100,6 +110,7 @@
     info = jnp.where(lane == 24, jnp.where(busy, j1 * NO + k1, -1).astype(F32), info)
     info = jnp.where(lane == 25, jnp.where(busy, j2 * NO + k2, -1).astype(F32), info)
     info = jnp.where(lane == 26, (trip_ref[1, 0, place] * NO + trip_ref[2, 0, place]).astype(F32), info)
+    info = jnp.where(lane == 27, diagonal.astype(F32), info)
     info_ref[...] = info
 
     sub = lax.broadcasted_iota(jnp.int32, (slots, 128), 0)
@@ -143,8 +154,7 @@
 def energy_kernel(ints_ref, one_ref, two_ref, recip_ref, amps_ref, info_ref, out_ref, sums_ref):
     occupied, width_block, width, _ = ints_ref.shape
     _, z, _, _, _ = where_am_i()
-    (j1, k1), _ = own_pairs()
-    diagonal = j1 == k1
+    diagonal = jnp.max(info_ref[:, 27:28]) > 0.5
     sums_ref[...] = jnp.zeros(sums_ref.shape, F32)
 
     def fold(value):
@@ -184,7 +194,7 @@
             sums_ref[pl.ds(i + occupied, 1), :] = jnp.sum(total_two, axis=0, keepdims=True)
             return carry
 
-        lax.fori_loop(0, occupied, one_occ, 0)
+        lax.fori_loop(0, occupied, one_occ, 0, unroll=True)
 
     busy = z < WORKERS
 
@@ -286,12 +296,12 @@
             pltpu.VMEM((slots, 128), F32),
             pltpu.VMEM((slots, 128), F32),
         ),
-        in_specs=spaces(pl.ANY, *[pltpu.SMEM] * 5, pltpu.VMEM),
+        in_specs=spaces(pl.ANY, *[pltpu.SMEM] * 6, pltpu.VMEM),
         out_specs=tuple(vmem(6)),
         scratch_shapes=[pltpu.SemaphoreType.DMA],
         compiler_params=SMALL,
         name="prep",
-    )(*left_in_hbm(integrals, lists), tile_count, *left_in_hbm(occ_energy, vir_energy, singles, vir_energy[None]))
+    )(*left_in_hbm(integrals, jnp.asarray(owner_table()), lists), tile_count, *left_in_hbm(occ_energy, vir_energy, singles, vir_energy[None]))
 
 
 def energy_call(slabs, one, two, recip, amps, info):
@@ -331,10 +341,10 @@
 
 
 def body(integrals, doubles, coulomb, singles, occ_energy, vir_energy, triplets, tile_count):
-    first, second = routes()
+    near, far = routes()
     sent = rows_call(doubles, coulomb)
-    one = lax.ppermute(sent, AXES, first)
-    two = lax.ppermute(sent, AXES, second)
+    two = lax.ppermute(sent, AXES, far)
+    one = lax.ppermute(sent, AXES, near)
     lists = jnp.transpose(triplets, (2, 0, 1))
     slabs, recip, amps, info, first_hot, pair_hot = prep_call(integrals, lists, tile_count, occ_energy, vir_energy, singles)
     message = energy_call(slabs, one, two, recip, amps, info)

time: 65.9 us -> 60.6 us (0.920)
  starting transfers between devices: 15.8 us -> 10.5 us
  blocking collectives: 37.1 us -> 40.2 us
  Pallas kernels: 8.5 us -> 6.35 us
  waiting for transfers between devices: 2.88 us -> 1.8 us
    all_to_all x1, blocking collectives: 16.1 us -> 22.4 us  [body(): message = lax.all_to_all(message, PLANE, 0, 0, tiled=True)]
    ppermute x2, starting transfers between devices: 15.8 us -> 10.5 us  [the longest x1 7.06 us: body(): two = lax.ppermute(sent, AXES, far)]
    all_to_all x1, blocking collectives: 21 us -> 17.7 us  [body(): tables = lax.all_to_all(tables, STACK, 0, 0, tiled=True)]
    pallas_call x1, Pallas kernels: 4.25 us -> 2.07 us  [energy_call(): pl.pallas_call(energy_kernel, out_shape=pltpu.VMEM((64, 128), F32), in_sp...]
    ppermute x2, waiting for transfers between devices: 2.88 us -> 1.8 us  [the longest x1 1.07 us: body(): two = lax.ppermute(sent, AXES, far)]
  transfers between devices with their start and end apart: 2 -> 2, of which waited for: 1 -> 2; matrix products, arithmetic and copies ran while one was open for 0% -> 0% of each run, Pallas kernels for 4% -> 4%
where the time goes in v4:
time: 60.6 us; the launch traced here: 60.2 us
  blocking collectives  40.2 us (66%)
  starting transfers between devices  10.5 us (17%)
  Pallas kernels  6.35 us (10%)
  waiting for transfers between devices  1.8 us (3%)
  between operations  1.32 us (2%)
    all_to_all x1, blocking collectives, body(): message = lax.all_to_all(message, PLANE, 0, 0, tiled=True)  22.4 us
    all_to_all x1, blocking collectives, body(): tables = lax.all_to_all(tables, STACK, 0, 0, tiled=True)  17.7 us
    ppermute x1, starting transfers between devices, body(): two = lax.ppermute(sent, AXES, far)  7.06 us
    ppermute x1, starting transfers between devices, body(): one = lax.ppermute(sent, AXES, near)  3.46 us
    pallas_call x1, Pallas kernels, prep_call(): pl.pallas_call(prep_kernel, out_shape=(pltpu.VMEM(integrals.shape, integr...  2.42 us
    pallas_call x1, Pallas kernels, energy_call(): pl.pallas_call(energy_kernel, out_shape=pltpu.VMEM((64, 128), F32), in_sp...  2.07 us
  transfers between devices with their start and end apart: 2, of which 2 were waited for; matrix products, arithmetic and copies ran while one was open for 0% of the time, Pallas kernels for 4%

profile of v4, /device:TPU:1, one launch (start us, length us, event | category | flops | bytes accessed | tf_op | source)
XLA Modules:
  0.0 60.2 jit_solution(8357387314600783926)
XLA Ops:
  0.6 0.8 %rows.1 = bf16[2,128,128]{2,1,0:T(8,128)(2,1)S(1)} custom-call(bf16[4,128,128]{2,1,0:T(8,128)(2,1)} %doubles_ref.1, bf16[4,128,128]{2,1,0:T(8,128)(2,1)} %coulomb_ref.1), custom_call_target="tpu_custom_call" | custom-call | tf_op jit(solution)/shard_map/rows/pallas_call | solution.py:274
  1.4 7.1 %collective-permute-start.1 = (bf16[2,128,128]{2,1,0:T(8,128)(2,1)S(1)}, bf16[2,128,128]{2,1,0:T(8,128)(2,1)S(1)}, u32[]{:S(2)}, u32[]{:S(2)}) collective-permute-start(bf16[2,128,128]{2,1,0:T(8,128)(2,1)S(1)} %rows.1), channel_id=1, source_target_pairs={{4,0},{0,1},{527,2},{526,3},{522,4},{520,5},{523,6},{524,7},{518,8... | collective-permute-start | bytes 196616 | tf_op jit(solution)/shard_map/ppermute | solution.py:346
  8.5 3.5 %collective-permute-start = (bf16[2,128,128]{2,1,0:T(8,128)(2,1)S(1)}, bf16[2,128,128]{2,1,0:T(8,128)(2,1)S(1)}, u32[]{:S(2)}, u32[]{:S(2)}) collective-permute-start(bf16[2,128,128]{2,1,0:T(8,128)(2,1)S(1)} %rows.1), channel_id=1, source_target_pairs={{6,0},{2,1},{525,2},{7,3},{3,4},{1,5},{521,6},{5,7},{514,8},{14,9}... | collective-permute-start | bytes 196616 | tf_op jit(solution)/shard_map/ppermute | solution.py:347
  12.6 2.4 %prep.1 = (bf16[8,8,128,128]{3,2,1,0:T(8,128)(2,1)S(1)}, f32[2,64,128,128]{3,2,1,0:T(8,128)S(1)}, f32[64,128]{1,0:T(8,128)S(1)}, f32[1,128]{1,0:T(1,128)S(1)}, f...) custom-call(bf16[8,8,128,128]{3,2,1,0:T(8,128)(2,1)} %ints_ref.1, s32[512]{0:T(512)} %constant.2.clone.owners_ref, ...), custom_call_target="tpu_custom_call" | custom-call | tf_op jit(solution)/shard_map/prep/pallas_call | solution.py:289
  15.1 1.1 %collective-permute-done.1.two_ref = bf16[2,128,128]{2,1,0:T(8,128)(2,1)S(1)} collective-permute-done((bf16[2,128,128]{2,1,0:T(8,128)(2,1)S(1)}, bf16[2,128,128]{2,1,0:T(8,128)(2,1)S(1)}, u32[]{:S(2)}, u32[]{:S(2)}) %collective-permute-start.1) | collective-permute-done | bytes 65568 | tf_op jit(solution)/shard_map/ppermute | solution.py:346
  16.1 0.7 %collective-permute-done.one_ref = bf16[2,128,128]{2,1,0:T(8,128)(2,1)S(1)} collective-permute-done((bf16[2,128,128]{2,1,0:T(8,128)(2,1)S(1)}, bf16[2,128,128]{2,1,0:T(8,128)(2,1)S(1)}, u32[]{:S(2)}, u32[]{:S(2)}) %collective-permute-start) | collective-permute-done | bytes 65568 | tf_op jit(solution)/shard_map/ppermute | solution.py:347
  16.9 2.1 %energies.1 = f32[64,128]{1,0:T(8,128)S(1)} custom-call(bf16[8,8,128,128]{3,2,1,0:T(8,128)(2,1)S(1)} %get-tuple-element.10.ints_ref, bf16[2,128,128]{2,1,0:T(8,128)(2,1)S(1)} %collective-permute-done.one_ref, bf16[2,128,128]{2,1,0:T(8,128)(2,1)S(1)} %collective-permute-done.1.two_ref, f32[2,64,128,128]{3,2,1,0:T(8,128)S(1)} %get-tuple-element.11.recip_ref, ...), custom_call_target="tpu_custom_call" | custom-call | tf_op jit(solution)/shard_map/energies/pallas_call | solution.py:309
  18.9 22.4 %all_to_all.22 = f32[64,1,128]{2,1,0:T(1,128)S(1)} all-to-all(f32[64,1,128]{2,1,0:T(1,128)S(1)} %bitcast.11), channel_id=1, replica_groups=mesh['yl'=4,'z'=8,'c'=2,'yh'=2,'x'=8] {'yh','yl','x'}, dimensions={0} | all-to-all | bytes 65536 | tf_op jit(solution)/shard_map/all_to_all | solution.py:351
  41.4 0.4 table.1
  41.7 17.7 %all_to_all.23 = f32[16,8,128]{2,1,0:T(8,128)S(1)} all-to-all(f32[16,8,128]{2,1,0:T(8,128)S(1)} %bitcast.10), channel_id=1, replica_groups=mesh['yl'=4,'z'=8,'c'=2,'yh'=2,'x'=8] {'z','c'}, dimensions={0} | all-to-all | bytes 131072 | tf_op jit(solution)/shard_map/all_to_all | solution.py:353
  59.5 0.7 %lookup.1 = (f32[1,16]{1,0:T(1,128)}, f32[1,1]{1,0:T(1,128)}) custom-call(f32[128,128]{1,0:T(8,128)S(1)} %bitcast.9, f32[16,128]{1,0:T(8,128)S(1)} %get-tuple-element.14.first_ref, f32[16,128]{1,0:T(8,128)S(1)} %get-tuple-element.15.pair_ref), custom_call_target="tpu_custom_call" | custom-call | tf_op jit(solution)/shard_map/lookup/pallas_call | solution.py:333
Async XLA Ops:
  1.4 14.7 %collective-permute-start.1 = (bf16[2,128,128]{2,1,0:T(8,128)(2,1)S(1)}, bf16[2,128,128]{2,1,0:T(8,128)(2,1)S(1)}, u32[]{:S(2)}, u32[]{:S(2)}) collective-permute-start(bf16[2,128,128]{2,1,0:T(8,128)(2,1)S(1)} %rows.1), channel_id=1, source_target_pairs={{4,0},{0,1},{527,2},{526,3},{522,4},{520,5},{523,6},{524,7},{518,8... | collective-permute-start | bytes 196616 | tf_op jit(solution)/shard_map/ppermute | solution.py:346
  8.5 8.3 %collective-permute-start = (bf16[2,128,128]{2,1,0:T(8,128)(2,1)S(1)}, bf16[2,128,128]{2,1,0:T(8,128)(2,1)S(1)}, u32[]{:S(2)}, u32[]{:S(2)}) collective-permute-start(bf16[2,128,128]{2,1,0:T(8,128)(2,1)S(1)} %rows.1), channel_id=1, source_target_pairs={{6,0},{2,1},{525,2},{7,3},{3,4},{1,5},{521,6},{5,7},{514,8},{14,9}... | collective-permute-start | bytes 196616 | tf_op jit(solution)/shard_map/ppermute | solution.py:347

commit v5 on v4

v5 whole, which is shorter than its diff:
```python
import jax
import jax.numpy as jnp
import numpy as np
from jax import lax
from jax.experimental import pallas as pl
from jax.experimental.pallas import tpu as pltpu
from jax.sharding import Mesh
from jax.sharding import PartitionSpec as P

AXES = ("yl", "z", "c", "yh", "x")
SIZES = (4, 8, 2, 2, 8)
GRP = ("yl", "z", "c")
BLK = ("yh", "x")
PLANE = ("yh", "yl", "x")
STACK = ("z", "c")
NO = 8
WORKERS = 4
SMALL = pltpu.CompilerParams(vmem_limit_bytes=12 * 1024 * 1024)
F32 = jnp.float32


def device_at(yl, z, c, yh, x):
    return ((((yl * 8) + z) * 2 + c) * 2 + yh) * 8 + x


OWNERS = (
    (0x1739dbf5ace48206, 0x5fd7b193c64e28a0, 0x3961705deaf24b8c, 0xf57d238960c1e4ba,
     0x74b25d310f8cae69, 0x93541706fe2dbac8, 0x0123456789abcdef, 0x6215347098badcfe),
    (0x7f5db1986e4c3a02, 0xf5dc3b1976e420a8, 0x50b317df928e46ca, 0x9475d031ecf2a8b6,
     0x471b5360fa2dce89, 0x89412d05afc3eb67, 0x0132457689abdcef, 0x1324c657089abdfe),
    (0xfb39d5e708a264c1, 0x9ad5bcfe12384706, 0x39ba5d1f8e24c670, 0x138b7fd9204a5c6e,
     0x58a23406f1c9ebd7, 0x21c46370df8ba5e9, 0x70234651a9bcdef8, 0x0241c765ea93bd8f),
    (0x73b91efdc20864a5, 0xdb679fc30a1e8542, 0xf97a6d15b324e8c0, 0x589b73d120a64fec,
     0x0152364f89bcaed7, 0x3210b7549ecaf68d, 0x10234567a89bcdfe, 0x2a315470eb89dc6f),
)
APART = 2


def owner_table():
    digits = [[[int(d, 16) for d in f"{code:016x}"] for code in codes] for codes in OWNERS]
    return np.array(digits, np.int32).reshape(-1)


def owner_index(yl, z, c, yh, x):
    return (((yl ^ (2 * yh)) * WORKERS + z % WORKERS) * 2 + c) * 16 + yh * 8 + x


def pairs_of(owner, u, where):
    swapped = ((owner & 1) << 3) | ((owner & 6) ^ (u << 1)) | (owner >> 3)
    other = where(swapped == owner, owner ^ APART, swapped)
    return other, pair_at(owner, u), pair_at(other, u)


def pair_at(owner, u):
    return owner >> 1, (owner & 1) * 4 + (((owner >> 1) & 3) ^ u)


def routes():
    table, near, far = owner_table(), [], []
    for yl, z, c, yh, x in np.ndindex(*SIZES):
        if z < WORKERS:
            here, u = device_at(yl, z, c, yh, x), yl ^ (2 * yh)
            owner = int(table[owner_index(yl, z, c, yh, x)])
            other, _, _ = pairs_of(owner, u, lambda a, b, c: b if a else c)
            for route, block in ((near, owner), (far, other)):
                half = block >> 3
                route.append((device_at(u ^ (2 * half), z, c, half, block & 7), here))
    return near, far


def where_am_i():
    yl, z, c, yh, x = (lax.axis_index(axis) for axis in AXES)
    return yl, z, c, yh, x


def rows_kernel(doubles_ref, coulomb_ref, out_ref, sems):
    yl, z, _, yh, x = where_am_i()
    row = (((yh * 8 + x) >> 1) & 3) ^ yl ^ (2 * yh)
    copies = [
        pltpu.make_async_copy(doubles_ref.at[row], out_ref.at[0], sems.at[0]),
        pltpu.make_async_copy(coulomb_ref.at[row], out_ref.at[1], sems.at[1]),
    ]

    @pl.when(z < WORKERS)
    def _():
        for copy in copies:
            copy.start()
        for copy in copies:
            copy.wait()


def prep_kernel(owners_ref, trip_ref, count_ref, occ_ref, vir_ref, singles_ref, virs_ref,
                recip_ref, amps_ref, info_ref, code_ref, slots_ref):
    occupied, width_block = singles_ref.shape
    width = virs_ref.shape[1]
    slots = trip_ref.shape[2]
    yl, z, c, yh, x = where_am_i()
    place = yh * 8 + x
    owner = owners_ref[owner_index(yl, z, c, yh, x)]
    other, (j1, k1), (j2, k2) = pairs_of(owner, yl ^ (2 * yh), jnp.where)
    diagonal = j1 == k1
    busy = z < WORKERS
    live = count_ref[0]

    lane = lax.broadcasted_iota(jnp.int32, (1, 128), 1)
    info = jnp.where(lane == 0, owner.astype(F32), 0.0)
    info = jnp.where(lane == 1, other.astype(F32), info)
    info_ref[...] = jnp.where(lane == 2, diagonal.astype(F32), info)

    def code_of(s):
        i, j, k = trip_ref[0, 0, s], trip_ref[1, 0, s], trip_ref[2, 0, s]
        code = ((j ^ k) & 3) * 128 + i * 16 + j * 2 + (k >> 2)
        return jnp.where(s < live, code, -1)

    code_ref[...] = jnp.where(lane == z * 2 + c, (code_of(place) + 1).astype(F32), 0.0)

    sub = lax.broadcasted_iota(jnp.int32, (slots, 128), 0)
    lanes = lax.broadcasted_iota(jnp.int32, (slots, 128), 1)
    codes = jnp.full((slots, 128), -1, jnp.int32)
    for s in range(slots):
        codes = jnp.where(sub == s, code_of(s), codes)
    for u in range(4):
        slots_ref[u] = jnp.where(codes == u * 128 + lanes, 1.0, 0.0)

    def fill(table, second, third, write_amps):
        across = jnp.broadcast_to(virs_ref[...], (width, width))
        sums = across.T + across

        def one_occ(i, carry):
            occ_sum = occ_ref[i] + occ_ref[second] + occ_ref[third]
            for a in range(width_block):
                r = i * width_block + a
                recip_ref[table, r] = 1.0 / ((occ_sum - vir_ref[place * width_block + a]) - sums)
                if write_amps:
                    amps_ref[pl.ds(r, 1), :] = jnp.full((1, 128), singles_ref[i, a], F32)
            return carry

        lax.fori_loop(0, occupied, one_occ, 0)

    @pl.when(busy)
    def _():
        fill(0, j1, k1, True)

    @pl.when(jnp.logical_and(busy, diagonal))
    def _():
        fill(1, j2, k2, False)


def energy_kernel(ints_ref, one_ref, two_ref, recip_ref, amps_ref, info_ref, code_ref, out_ref, sums_ref):
    occupied, width_block, width, _ = ints_ref.shape
    _, z, _, _, _ = where_am_i()
    diagonal = jnp.max(info_ref[:, 2:3]) > 0.5
    sums_ref[...] = jnp.zeros(sums_ref.shape, F32)

    def fold(value):
        return jnp.sum(value.reshape(width // 8, 8, width), axis=0)

    def both(couple):
        amps = jnp.concatenate([one_ref[0], two_ref[0]], axis=0)
        coupling_one = one_ref[1].astype(F32)
        coupling_two = two_ref[1].astype(F32)
        if couple:
            coupling_two = coupling_two.T

        def one_occ(i, carry):
            slab = ints_ref[i].reshape(width_block * width, width)
            products = lax.dot_general(slab, amps, (((1,), (1,)), ((), ())), preferred_element_type=F32)
            total_one = jnp.zeros((8, width), F32)
            total_two = jnp.zeros((8, width), F32)
            for a in range(width_block):
                r = i * width_block + a
                left = products[a * width:(a + 1) * width, :width]
                right = products[a * width:(a + 1) * width, width:]
                amp = amps_ref[pl.ds(r, 1), :]
                recip_one = recip_ref[0, r]
                if couple:
                    connected_one = right + left.T
                    connected_two = connected_one
                    recip_two = recip_one
                else:
                    connected_one = left + left.T
                    connected_two = right + right.T
                    recip_two = recip_ref[1, r]
                full_one = connected_one + amp * coupling_one
                full_two = connected_two + amp * coupling_two
                total_one = total_one + fold(full_one * full_one * recip_one)
                total_two = total_two + fold(full_two * full_two * recip_two)
            sums_ref[pl.ds(i, 1), :] = jnp.sum(total_one, axis=0, keepdims=True)
            sums_ref[pl.ds(i + occupied, 1), :] = jnp.sum(total_two, axis=0, keepdims=True)
            return carry

        lax.fori_loop(0, occupied, one_occ, 0, unroll=True)

    busy = z < WORKERS

    @pl.when(jnp.logical_and(busy, jnp.logical_not(diagonal)))
    def _():
        both(True)

    @pl.when(jnp.logical_and(busy, diagonal))
    def _():
        both(False)

    energies = jnp.sum(sums_ref[...], axis=1, keepdims=True)
    sub = lax.broadcasted_iota(jnp.int32, (2 * occupied, 128), 0)
    lane = lax.broadcasted_iota(jnp.int32, (2 * occupied, 128), 1)
    block = jnp.where(sub < occupied, info_ref[:, 0:1], info_ref[:, 1:2])
    there = (sub & (occupied - 1)).astype(F32) * 16.0 + block == lane.astype(F32)
    row = jnp.sum(jnp.where(there, energies, 0.0), axis=0, keepdims=True)
    both_rows = jnp.concatenate([row, code_ref[...]], axis=0)
    out_ref[...] = jnp.broadcast_to(both_rows[None], out_ref.shape)


def column_kernel(in_ref, out_ref):
    out_ref[...] = jnp.broadcast_to(jnp.sum(in_ref[...], axis=0, keepdims=True), out_ref.shape)


def final_kernel(in_ref, slots_ref, trip_ref, mean_ref):
    slots = slots_ref.shape[1]
    tables = in_ref[:, 0, :]
    codes = in_ref[:, 1, :] - 1.0
    lane = lax.broadcasted_iota(jnp.int32, codes.shape, 1).astype(F32)
    chosen = jnp.zeros((slots, 128), F32)
    total = jnp.zeros((8, 128), F32)
    columns = [jnp.broadcast_to(codes[:, n:n + 1], codes.shape) - lane for n in range(16)]
    for u in range(4):
        table = tables[u * 8:u * 8 + 8] + tables[(4 + (u ^ 2)) * 8:(4 + (u ^ 2)) * 8 + 8]
        table = jnp.sum(table, axis=0, keepdims=True)
        count = jnp.zeros(codes.shape, F32)
        for column in columns:
            count = count + jnp.where(column == u * 128.0, 1.0, 0.0)
        total = total + jnp.sum(count.reshape(8, 8, 128), axis=0) * table
        chosen = chosen + slots_ref[u] * table
    total = jnp.sum(total, axis=0, keepdims=True)
    mean_ref[...] = jnp.sum(total, axis=1, keepdims=True) / 1024.0
    values = jnp.sum(chosen, axis=1, keepdims=True)
    sub = lax.broadcasted_iota(jnp.int32, (slots, 128), 0)
    lanes = lax.broadcasted_iota(jnp.int32, (slots, 128), 1)
    row = jnp.sum(jnp.where(sub == lanes, values, 0.0), axis=0, keepdims=True)
    trip_ref[...] = row[:, :slots]


def spaces(*kinds):
    return [pl.BlockSpec(memory_space=kind) for kind in kinds]


def vmem(count):
    return spaces(*[pltpu.VMEM] * count)


def kept(*arrays):
    return [pltpu.with_memory_space_constraint(a, pltpu.VMEM) for a in arrays]


def left_in_hbm(*arrays):
    return [pltpu.with_memory_space_constraint(a, pltpu.HBM) for a in arrays]


def rows_call(doubles, coulomb):
    _, width, depth = doubles.shape
    return pl.pallas_call(
        rows_kernel,
        out_shape=pltpu.VMEM((2, width, depth), doubles.dtype),
        in_specs=spaces(pl.ANY, pl.ANY),
        out_specs=vmem(1)[0],
        scratch_shapes=[pltpu.SemaphoreType.DMA((2,))],
        compiler_params=SMALL,
        cost_estimate=pl.CostEstimate(flops=10**9, bytes_accessed=2**20, transcendentals=0),
        name="rows",
    )(*left_in_hbm(doubles, coulomb))


def prep_call(lists, tile_count, occ_energy, vir_energy, singles):
    occupied, width_block = singles.shape
    width = vir_energy.shape[0]
    slots = lists.shape[2]
    return pl.pallas_call(
        prep_kernel,
        out_shape=(
            pltpu.VMEM((2, occupied * width_block, width, width), F32),
            pltpu.VMEM((occupied * width_block, width), F32),
            pltpu.VMEM((1, 128), F32),
            pltpu.VMEM((1, 128), F32),
            pltpu.VMEM((4, slots, 128), F32),
        ),
        in_specs=spaces(*[pltpu.SMEM] * 6, pltpu.VMEM),
        out_specs=tuple(vmem(5)),
        compiler_params=SMALL,
        cost_estimate=pl.CostEstimate(flops=10**10, bytes_accessed=16 * 2**20, transcendentals=2**22),
        name="prep",
    )(*left_in_hbm(jnp.asarray(owner_table()), lists), tile_count, *left_in_hbm(occ_energy, vir_energy, singles, vir_energy[None]))


def energy_call(integrals, one, two, recip, amps, info, code):
    occupied, _, width, _ = integrals.shape
    return pl.pallas_call(
        energy_kernel,
        out_shape=pltpu.VMEM((16, 2, 128), F32),
        in_specs=vmem(7),
        out_specs=vmem(1)[0],
        scratch_shapes=[pltpu.VMEM((2 * occupied, width), F32)],
        compiler_params=SMALL,
        name="energies",
    )(*kept(integrals, one, two, recip, amps, info, code))


def column_call(rows):
    return pl.pallas_call(
        column_kernel,
        out_shape=pltpu.VMEM((64, 2, 128), F32),
        in_specs=vmem(1),
        out_specs=vmem(1)[0],
        compiler_params=SMALL,
        name="column",
    )(*kept(rows))


def final_call(rows, slot_masks):
    slots = slot_masks.shape[1]
    return pl.pallas_call(
        final_kernel,
        out_shape=(jax.ShapeDtypeStruct((1, slots), F32), jax.ShapeDtypeStruct((1, 1), F32)),
        in_specs=vmem(2),
        out_specs=tuple(vmem(2)),
        compiler_params=SMALL,
        name="lookup",
    )(*kept(rows, slot_masks))


def body(integrals, doubles, coulomb, singles, occ_energy, vir_energy, triplets, tile_count):
    near, far = routes()
    sent = rows_call(doubles, coulomb)
    two = lax.ppermute(sent, AXES, far)
    one = lax.ppermute(sent, AXES, near)
    lists = jnp.transpose(triplets, (2, 0, 1))
    recip, amps, info, code, slot_masks = prep_call(lists, tile_count, occ_energy, vir_energy, singles)
    rows = energy_call(integrals, one, two, recip, amps, info, code)
    rows = lax.all_to_all(rows, STACK, 0, 0, tiled=True)
    rows = lax.all_to_all(column_call(rows), PLANE, 0, 0, tiled=True)
    trip, mean = final_call(rows, slot_masks)
    return trip, mean.reshape(())


def solution(mesh):
    fine = Mesh(mesh.devices.reshape(SIZES), AXES)
    in_specs = (
        P(None, BLK, None, None),
        P(BLK, None, None),
        P(BLK, None, None),
        P(None, BLK),
        P(),
        P(),
        P(GRP, None, None),
        P(GRP),
    )
    out_specs = (P(GRP, None), P())
    return jax.shard_map(body, mesh=fine, in_specs=in_specs, out_specs=out_specs, check_vma=False)
```

time: 60.6 us -> 59.6 us (0.983)
  blocking collectives: 40.2 us -> 33.4 us
  starting transfers between devices: 10.5 us -> 14.2 us
  waiting for transfers between devices: 1.8 us -> 3.72 us
    all_to_all x2, blocking collectives: 40.2 us -> 33.4 us  [the longest x1 20.8 us: body(): rows = lax.all_to_all(column_call(rows), PLANE, 0, 0, tiled=True)]
    ppermute x1, starting transfers between devices: 7.06 us -> 12.3 us  [body(): two = lax.ppermute(sent, AXES, far)]
    ppermute x1, waiting for transfers between devices: 0.73 us -> 3.72 us  [body(): one = lax.ppermute(sent, AXES, near)]
    ppermute x1, starting transfers between devices: 3.46 us -> 1.92 us  [body(): one = lax.ppermute(sent, AXES, near)]
    pallas_call x1, Pallas kernels: 0.69 us -> 1.82 us  [final_call(): pl.pallas_call(final_kernel, out_shape=(jax.ShapeDtypeStruct((1, slots),...]
    ppermute x1, waiting for transfers between devices: 1.07 us -> 0.01 us  [body(): two = lax.ppermute(sent, AXES, far)]
    pallas_call x3, Pallas kernels: 4.86 us -> 3.98 us  [the longest x1 2.14 us: energy_call(): pl.pallas_call(energy_kernel, out_shape=pltpu.VMEM((16, 2, 128), F32), in...]
  transfers between devices with their start and end apart: 2 -> 2, of which waited for: 2 -> 1; matrix products, arithmetic and copies ran while one was open for 0% -> 0% of each run, Pallas kernels for 4% -> 3%
where the time goes in v5:
time: 59.6 us; the launch traced here: 59.3 us
  blocking collectives  33.4 us (56%)
  starting transfers between devices  14.2 us (24%)
  Pallas kernels  6.61 us (11%)
  waiting for transfers between devices  3.72 us (6%)
  between operations  1.34 us (2%)
    all_to_all x1, blocking collectives, body(): rows = lax.all_to_all(column_call(rows), PLANE, 0, 0, tiled=True)  20.8 us
    all_to_all x1, blocking collectives, body(): rows = lax.all_to_all(rows, STACK, 0, 0, tiled=True)  12.5 us
    ppermute x1, starting transfers between devices, body(): two = lax.ppermute(sent, AXES, far)  12.3 us
    ppermute x1, waiting for transfers between devices, body(): one = lax.ppermute(sent, AXES, near)  3.72 us
    pallas_call x1, Pallas kernels, energy_call(): pl.pallas_call(energy_kernel, out_shape=pltpu.VMEM((16, 2, 128), F32), in...  2.14 us
    ppermute x1, starting transfers between devices, body(): one = lax.ppermute(sent, AXES, near)  1.92 us
    pallas_call x1, Pallas kernels, final_call(): pl.pallas_call(final_kernel, out_shape=(jax.ShapeDtypeStruct((1, slots),...  1.82 us
    pallas_call x1, Pallas kernels, prep_call(): pl.pallas_call(prep_kernel, out_shape=(pltpu.VMEM((2, occupied * width_bl...  1.8 us
  transfers between devices with their start and end apart: 2, of which 1 were waited for; matrix products, arithmetic and copies ran while one was open for 0% of the time, Pallas kernels for 3%

profile of v5, /device:TPU:1, one launch (start us, length us, event | category | flops | bytes accessed | tf_op | source)
XLA Modules:
  0.0 59.3 jit_solution(6726957443008229175)
XLA Ops:
  0.6 0.8 %rows.1 = bf16[2,128,128]{2,1,0:T(8,128)(2,1)S(1)} custom-call(bf16[4,128,128]{2,1,0:T(8,128)(2,1)} %doubles_ref.1, bf16[4,128,128]{2,1,0:T(8,128)(2,1)} %coulomb_ref.1), custom_call_target="tpu_custom_call" | custom-call | flops 1000000000 | bytes 1048576 | tf_op jit(solution)/shard_map/rows/pallas_call | solution.py:261
  1.4 12.3 %collective-permute-start.1 = (bf16[2,128,128]{2,1,0:T(8,128)(2,1)S(1)}, bf16[2,128,128]{2,1,0:T(8,128)(2,1)S(1)}, u32[]{:S(2)}, u32[]{:S(2)}) collective-permute-start(bf16[2,128,128]{2,1,0:T(8,128)(2,1)S(1)} %rows.1), channel_id=1, source_target_pairs={{520,0},{526,1},{522,2},{523,3},{527,4},{521,5},{525,6},{524,7},{5... | collective-permute-start | bytes 196616 | tf_op jit(solution)/shard_map/ppermute | solution.py:333
  13.8 1.9 %collective-permute-start = (bf16[2,128,128]{2,1,0:T(8,128)(2,1)S(1)}, bf16[2,128,128]{2,1,0:T(8,128)(2,1)S(1)}, u32[]{:S(2)}, u32[]{:S(2)}) collective-permute-start(bf16[2,128,128]{2,1,0:T(8,128)(2,1)S(1)} %rows.1), channel_id=1, source_target_pairs={{1,0},{7,1},{3,2},{521,3},{525,4},{523,5},{527,6},{5,7},{512,8},{8... | collective-permute-start | bytes 196616 | tf_op jit(solution)/shard_map/ppermute | solution.py:334
  16.3 0.0 copy-start
  16.3 1.8 %prep.1 = (f32[2,64,128,128]{3,2,1,0:T(8,128)S(1)}, f32[64,128]{1,0:T(8,128)S(1)}, f32[1,128]{1,0:T(1,128)S(1)}, f32[1,128]{1,0:T(1,128)S(1)}, f32[4,16,128]{2,1,0:T(8,128)S(1)}) custom-call(s32[512]{0:T(512)} %constant.2.clone.owners_ref, s32[3,1,16]{2,1,0:T(1,128)} %bitcast.3, s32[1]{0:T(128)S(6)} %copy.11.count_ref, f32[8]{0:T(128)} %occ_ref.1, ...), custom_call_target="tpu_custom_call" | custom-call | flops 10000000000 | bytes 16777216 | tf_op jit(solution)/shard_map/prep/pallas_call | solution.py:277
  18.1 0.0 collective-permute-done.1.two_ref
  18.2 3.7 %collective-permute-done.one_ref = bf16[2,128,128]{2,1,0:T(8,128)(2,1)S(1)} collective-permute-done((bf16[2,128,128]{2,1,0:T(8,128)(2,1)S(1)}, bf16[2,128,128]{2,1,0:T(8,128)(2,1)S(1)}, u32[]{:S(2)}, u32[]{:S(2)}) %collective-permute-start) | collective-permute-done | bytes 65568 | tf_op jit(solution)/shard_map/ppermute | solution.py:334
  21.9 0.0 copy-done
  21.9 2.1 %energies.1 = f32[16,2,128]{2,1,0:T(2,128)S(1)} custom-call(bf16[8,8,128,128]{3,2,1,0:T(8,128)(2,1)S(1)} %copy-done, bf16[2,128,128]{2,1,0:T(8,128)(2,1)S(1)} %collective-permute-done.one_ref, bf16[2,128,128]{2,1,0:T(8,128)(2,1)S(1)} %collective-permute-done.1.two_ref, f32[2,64,128,128]{3,2,1,0:T(8,128)S(1)} %get-tuple-element.9.recip_ref, ...), custom_call_target="tpu_custom_call" | custom-call | tf_op jit(solution)/shard_map/energies/pallas_call | solution.py:296
  24.0 12.5 %all_to_all.10.in_ref = f32[16,2,128]{2,1,0:T(2,128)S(1)} all-to-all(f32[16,2,128]{2,1,0:T(2,128)S(1)} %energies.1), channel_id=1, replica_groups=mesh['yl'=4,'z'=8,'c'=2,'yh'=2,'x'=8] {'z','c'}, dimensions={0} | all-to-all | bytes 32768 | tf_op jit(solution)/shard_map/all_to_all | solution.py:338
  36.6 20.8 %all_to_all.11.in_ref = f32[64,2,128]{2,1,0:T(2,128)S(1)} all-to-all(f32[64,2,128]{2,1,0:T(2,128)S(1)} %column.1), channel_id=1, replica_groups=mesh['yl'=4,'z'=8,'c'=2,'yh'=2,'x'=8] {'yh','yl','x'}, dimensions={0} | all-to-all | bytes 131072 | tf_op jit(solution)/shard_map/all_to_all | solution.py:339
  57.4 1.8 %lookup.1 = (f32[1,16]{1,0:T(1,128)}, f32[1,1]{1,0:T(1,128)}) custom-call(f32[64,2,128]{2,1,0:T(2,128)S(1)} %all_to_all.11.in_ref, f32[4,16,128]{2,1,0:T(8,128)S(1)} %get-tuple-element.13.slots_ref), custom_call_target="tpu_custom_call" | custom-call | tf_op jit(solution)/shard_map/lookup/pallas_call | solution.py:320
  (1 shorter events, 0.0 us)
Async XLA Ops:
  1.4 16.7 %collective-permute-start.1 = (bf16[2,128,128]{2,1,0:T(8,128)(2,1)S(1)}, bf16[2,128,128]{2,1,0:T(8,128)(2,1)S(1)}, u32[]{:S(2)}, u32[]{:S(2)}) collective-permute-start(bf16[2,128,128]{2,1,0:T(8,128)(2,1)S(1)} %rows.1), channel_id=1, source_target_pairs={{520,0},{526,1},{522,2},{523,3},{527,4},{521,5},{525,6},{524,7},{5... | collective-permute-start | bytes 196616 | tf_op jit(solution)/shard_map/ppermute | solution.py:333
  13.8 8.1 %collective-permute-start = (bf16[2,128,128]{2,1,0:T(8,128)(2,1)S(1)}, bf16[2,128,128]{2,1,0:T(8,128)(2,1)S(1)}, u32[]{:S(2)}, u32[]{:S(2)}) collective-permute-start(bf16[2,128,128]{2,1,0:T(8,128)(2,1)S(1)} %rows.1), channel_id=1, source_target_pairs={{1,0},{7,1},{3,2},{521,3},{525,4},{523,5},{527,6},{5,7},{512,8},{8... | collective-permute-start | bytes 196616 | tf_op jit(solution)/shard_map/ppermute | solution.py:334
  16.3 5.5 %copy-start = (bf16[8,8,128,128]{3,2,1,0:T(8,128)(2,1)S(1)}, bf16[8,8,128,128]{3,2,1,0:T(8,128)(2,1)}, u32[]{:S(2)}) copy-start(bf16[8,8,128,128]{3,2,1,0:T(8,128)(2,1)} %ints_ref.1) | copy-start | bytes 6291460

commit v6 on v5

--- a/solution.py
+++ b/solution.py
@@ -207,29 +207,34 @@
     block = jnp.where(sub < occupied, info_ref[:, 0:1], info_ref[:, 1:2])
     there = (sub & (occupied - 1)).astype(F32) * 16.0 + block == lane.astype(F32)
     row = jnp.sum(jnp.where(there, energies, 0.0), axis=0, keepdims=True)
-    both_rows = jnp.concatenate([row, code_ref[...]], axis=0)
-    out_ref[...] = jnp.broadcast_to(both_rows[None], out_ref.shape)
+    even = lax.broadcasted_iota(jnp.int32, out_ref.shape, 0) % 2 == 0
+    out_ref[...] = jnp.where(even, row, code_ref[...])
 
 
 def column_kernel(in_ref, out_ref):
-    out_ref[...] = jnp.broadcast_to(jnp.sum(in_ref[...], axis=0, keepdims=True), out_ref.shape)
+    total = jnp.sum(in_ref[...].reshape(4, 8, 128), axis=0)
+    total = total + pltpu.roll(total, 4, 0)
+    total = total + pltpu.roll(total, 2, 0)
+    out_ref[...] = jnp.broadcast_to(total[None], (16, 8, 128)).reshape(128, 128)
 
 
 def final_kernel(in_ref, slots_ref, trip_ref, mean_ref):
     slots = slots_ref.shape[1]
-    tables = in_ref[:, 0, :]
-    codes = in_ref[:, 1, :] - 1.0
-    lane = lax.broadcasted_iota(jnp.int32, codes.shape, 1).astype(F32)
+    lane = lax.broadcasted_iota(jnp.int32, (8, 128), 1).astype(F32) + 1.0
+    counts = [jnp.zeros((8, 128), F32) for _ in range(4)]
+    tables = []
+    for q in range(8):
+        tables.append(in_ref[pl.ds(16 * q, 8, 2), :])
+        codes = in_ref[pl.ds(16 * q + 1, 8, 2), :]
+        for n in range(16):
+            column = jnp.broadcast_to(codes[:, n:n + 1], (8, 128)) - lane
+            for u in range(4):
+                counts[u] = counts[u] + jnp.where(column == u * 128.0, 1.0, 0.0)
     chosen = jnp.zeros((slots, 128), F32)
     total = jnp.zeros((8, 128), F32)
-    columns = [jnp.broadcast_to(codes[:, n:n + 1], codes.shape) - lane for n in range(16)]
     for u in range(4):
-        table = tables[u * 8:u * 8 + 8] + tables[(4 + (u ^ 2)) * 8:(4 + (u ^ 2)) * 8 + 8]
-        table = jnp.sum(table, axis=0, keepdims=True)
-        count = jnp.zeros(codes.shape, F32)
-        for column in columns:
-            count = count + jnp.where(column == u * 128.0, 1.0, 0.0)
-        total = total + jnp.sum(count.reshape(8, 8, 128), axis=0) * table
+        table = jnp.sum(tables[u] + tables[4 + (u ^ 2)], axis=0, keepdims=True)
+        total = total + counts[u] * table
         chosen = chosen + slots_ref[u] * table
     total = jnp.sum(total, axis=0, keepdims=True)
     mean_ref[...] = jnp.sum(total, axis=1, keepdims=True) / 1024.0
@@ -295,7 +300,7 @@
     occupied, _, width, _ = integrals.shape
     return pl.pallas_call(
         energy_kernel,
-        out_shape=pltpu.VMEM((16, 2, 128), F32),
+        out_shape=pltpu.VMEM((32, 128), F32),
         in_specs=vmem(7),
         out_specs=vmem(1)[0],
         scratch_shapes=[pltpu.VMEM((2 * occupied, width), F32)],
@@ -307,7 +312,7 @@
 def column_call(rows):
     return pl.pallas_call(
         column_kernel,
-        out_shape=pltpu.VMEM((64, 2, 128), F32),
+        out_shape=pltpu.VMEM((128, 128), F32),
         in_specs=vmem(1),
         out_specs=vmem(1)[0],
         compiler_params=SMALL,

time: 59.6 us -> 58.6 us (0.983)
  Pallas kernels: 6.61 us -> 5.65 us
    pallas_call x1, Pallas kernels: 1.82 us -> 0.9 us  [final_call(): pl.pallas_call(final_kernel, out_shape=(jax.ShapeDtypeStruct((1, slots),...]
where the time goes in v6:
time: 58.6 us; the launch traced here: 58.3 us
  blocking collectives  33.4 us (57%)
  starting transfers between devices  14.2 us (24%)
  Pallas kernels  5.65 us (10%)
  waiting for transfers between devices  3.72 us (6%)
  between operations  1.33 us (2%)
    all_to_all x1, blocking collectives, body(): rows = lax.all_to_all(column_call(rows), PLANE, 0, 0, tiled=True)  20.8 us
    all_to_all x1, blocking collectives, body(): rows = lax.all_to_all(rows, STACK, 0, 0, tiled=True)  12.5 us
    ppermute x1, starting transfers between devices, body(): two = lax.ppermute(sent, AXES, far)  12.3 us
    ppermute x1, waiting for transfers between devices, body(): one = lax.ppermute(sent, AXES, near)  3.72 us
    pallas_call x1, Pallas kernels, energy_call(): pl.pallas_call(energy_kernel, out_shape=pltpu.VMEM((32, 128), F32), in_sp...  2.13 us
    ppermute x1, starting transfers between devices, body(): one = lax.ppermute(sent, AXES, near)  1.92 us
    pallas_call x1, Pallas kernels, prep_call(): pl.pallas_call(prep_kernel, out_shape=(pltpu.VMEM((2, occupied * width_bl...  1.8 us
  transfers between devices with their start and end apart: 2, of which 1 were waited for; matrix products, arithmetic and copies ran while one was open for 0% of the time, Pallas kernels for 3%

profile of v6, /device:TPU:1, one launch (start us, length us, event | category | flops | bytes accessed | tf_op | source)
XLA Modules:
  0.0 58.3 jit_solution(1366190096027213040)
XLA Ops:
  0.6 0.8 %rows.1 = bf16[2,128,128]{2,1,0:T(8,128)(2,1)S(1)} custom-call(bf16[4,128,128]{2,1,0:T(8,128)(2,1)} %doubles_ref.1, bf16[4,128,128]{2,1,0:T(8,128)(2,1)} %coulomb_ref.1), custom_call_target="tpu_custom_call" | custom-call | flops 1000000000 | bytes 1048576 | tf_op jit(solution)/shard_map/rows/pallas_call | solution.py:266
  1.4 12.3 %collective-permute-start.1 = (bf16[2,128,128]{2,1,0:T(8,128)(2,1)S(1)}, bf16[2,128,128]{2,1,0:T(8,128)(2,1)S(1)}, u32[]{:S(2)}, u32[]{:S(2)}) collective-permute-start(bf16[2,128,128]{2,1,0:T(8,128)(2,1)S(1)} %rows.1), channel_id=1, source_target_pairs={{520,0},{526,1},{522,2},{523,3},{527,4},{521,5},{525,6},{524,7},{5... | collective-permute-start | bytes 196616 | tf_op jit(solution)/shard_map/ppermute | solution.py:338
  13.8 1.9 %collective-permute-start = (bf16[2,128,128]{2,1,0:T(8,128)(2,1)S(1)}, bf16[2,128,128]{2,1,0:T(8,128)(2,1)S(1)}, u32[]{:S(2)}, u32[]{:S(2)}) collective-permute-start(bf16[2,128,128]{2,1,0:T(8,128)(2,1)S(1)} %rows.1), channel_id=1, source_target_pairs={{1,0},{7,1},{3,2},{521,3},{525,4},{523,5},{527,6},{5,7},{512,8},{8... | collective-permute-start | bytes 196616 | tf_op jit(solution)/shard_map/ppermute | solution.py:339
  16.3 0.0 copy-start
  16.3 1.8 %prep.1 = (f32[2,64,128,128]{3,2,1,0:T(8,128)S(1)}, f32[64,128]{1,0:T(8,128)S(1)}, f32[1,128]{1,0:T(1,128)S(1)}, f32[1,128]{1,0:T(1,128)S(1)}, f32[4,16,128]{2,1,0:T(8,128)S(1)}) custom-call(s32[512]{0:T(512)} %constant.2.clone.owners_ref, s32[3,1,16]{2,1,0:T(1,128)} %bitcast.11, s32[1]{0:T(128)S(6)} %copy.11.count_ref, f32[8]{0:T(128)} %occ_ref.1, ...), custom_call_target="tpu_custom_call" | custom-call | flops 10000000000 | bytes 16777216 | tf_op jit(solution)/shard_map/prep/pallas_call | solution.py:282
  18.1 0.0 collective-permute-done.1.two_ref
  18.2 3.7 %collective-permute-done.one_ref = bf16[2,128,128]{2,1,0:T(8,128)(2,1)S(1)} collective-permute-done((bf16[2,128,128]{2,1,0:T(8,128)(2,1)S(1)}, bf16[2,128,128]{2,1,0:T(8,128)(2,1)S(1)}, u32[]{:S(2)}, u32[]{:S(2)}) %collective-permute-start) | collective-permute-done | bytes 65568 | tf_op jit(solution)/shard_map/ppermute | solution.py:339
  21.9 0.0 copy-done
  21.9 2.1 %energies.1 = f32[32,128]{1,0:T(8,128)S(1)} custom-call(bf16[8,8,128,128]{3,2,1,0:T(8,128)(2,1)S(1)} %copy-done, bf16[2,128,128]{2,1,0:T(8,128)(2,1)S(1)} %collective-permute-done.one_ref, bf16[2,128,128]{2,1,0:T(8,128)(2,1)S(1)} %collective-permute-done.1.two_ref, f32[2,64,128,128]{3,2,1,0:T(8,128)S(1)} %get-tuple-element.9.recip_ref, ...), custom_call_target="tpu_custom_call" | custom-call | tf_op jit(solution)/shard_map/energies/pallas_call | solution.py:301
  24.0 12.5 %all_to_all.22 = f32[16,2,128]{2,1,0:T(2,128)S(1)} all-to-all(f32[16,2,128]{2,1,0:T(2,128)S(1)} %bitcast.9), channel_id=1, replica_groups=mesh['yl'=4,'z'=8,'c'=2,'yh'=2,'x'=8] {'z','c'}, dimensions={0} | all-to-all | bytes 32768 | tf_op jit(solution)/shard_map/all_to_all | solution.py:343
  36.6 20.8 %all_to_all.23 = f32[64,2,128]{2,1,0:T(2,128)S(1)} all-to-all(f32[64,2,128]{2,1,0:T(2,128)S(1)} %bitcast.7), channel_id=1, replica_groups=mesh['yl'=4,'z'=8,'c'=2,'yh'=2,'x'=8] {'yh','yl','x'}, dimensions={0} | all-to-all | bytes 131072 | tf_op jit(solution)/shard_map/all_to_all | solution.py:344
  57.4 0.9 %lookup.1 = (f32[1,16]{1,0:T(1,128)}, f32[1,1]{1,0:T(1,128)}) custom-call(f32[128,128]{1,0:T(8,128)S(1)} %bitcast.8, f32[4,16,128]{2,1,0:T(8,128)S(1)} %get-tuple-element.13.slots_ref), custom_call_target="tpu_custom_call" | custom-call | tf_op jit(solution)/shard_map/lookup/pallas_call | solution.py:325
  (1 shorter events, 0.0 us)
Async XLA Ops:
  1.4 16.7 %collective-permute-start.1 = (bf16[2,128,128]{2,1,0:T(8,128)(2,1)S(1)}, bf16[2,128,128]{2,1,0:T(8,128)(2,1)S(1)}, u32[]{:S(2)}, u32[]{:S(2)}) collective-permute-start(bf16[2,128,128]{2,1,0:T(8,128)(2,1)S(1)} %rows.1), channel_id=1, source_target_pairs={{520,0},{526,1},{522,2},{523,3},{527,4},{521,5},{525,6},{524,7},{5... | collective-permute-start | bytes 196616 | tf_op jit(solution)/shard_map/ppermute | solution.py:338
  13.8 8.1 %collective-permute-start = (bf16[2,128,128]{2,1,0:T(8,128)(2,1)S(1)}, bf16[2,128,128]{2,1,0:T(8,128)(2,1)S(1)}, u32[]{:S(2)}, u32[]{:S(2)}) collective-permute-start(bf16[2,128,128]{2,1,0:T(8,128)(2,1)S(1)} %rows.1), channel_id=1, source_target_pairs={{1,0},{7,1},{3,2},{521,3},{525,4},{523,5},{527,6},{5,7},{512,8},{8... | collective-permute-start | bytes 196616 | tf_op jit(solution)/shard_map/ppermute | solution.py:339
  16.3 5.5 %copy-start = (bf16[8,8,128,128]{3,2,1,0:T(8,128)(2,1)S(1)}, bf16[8,8,128,128]{3,2,1,0:T(8,128)(2,1)}, u32[]{:S(2)}) copy-start(bf16[8,8,128,128]{3,2,1,0:T(8,128)(2,1)} %ints_ref.1) | copy-start | bytes 6291460

commit v7 on v6

--- a/solution.py
+++ b/solution.py
@@ -24,16 +24,16 @@
 
 
 OWNERS = (
-    (0x1739dbf5ace48206, 0x5fd7b193c64e28a0, 0x3961705deaf24b8c, 0xf57d238960c1e4ba,
-     0x74b25d310f8cae69, 0x93541706fe2dbac8, 0x0123456789abcdef, 0x6215347098badcfe),
-    (0x7f5db1986e4c3a02, 0xf5dc3b1976e420a8, 0x50b317df928e46ca, 0x9475d031ecf2a8b6,
-     0x471b5360fa2dce89, 0x89412d05afc3eb67, 0x0132457689abdcef, 0x1324c657089abdfe),
-    (0xfb39d5e708a264c1, 0x9ad5bcfe12384706, 0x39ba5d1f8e24c670, 0x138b7fd9204a5c6e,
-     0x58a23406f1c9ebd7, 0x21c46370df8ba5e9, 0x70234651a9bcdef8, 0x0241c765ea93bd8f),
-    (0x73b91efdc20864a5, 0xdb679fc30a1e8542, 0xf97a6d15b324e8c0, 0x589b73d120a64fec,
-     0x0152364f89bcaed7, 0x3210b7549ecaf68d, 0x10234567a89bcdfe, 0x2a315470eb89dc6f),
+    (0x1975dbf3ec0284a6, 0xf58db139c7e4620a, 0xeb947d1562c8a3f0, 0x5ab713df902e486c,
+     0x20315476af9bdc8e, 0x365b27410a8defc9, 0x01234567f9bacde8, 0x9742365081acbedf),
+    (0xf5bda1897c4e3602, 0x7fdc3b9856e420a1, 0x5943b7f160d2eac8, 0x9475d21f0e3ca8b6,
+     0x401b2d56fa93ce87, 0x8751c30eaf2d4b69, 0x0132456789cabdef, 0x1324567098abdcfe),
+    (0x39ba7df1e2485c60, 0x1f395b7d8ea0264c, 0x9751b3df602ac48e, 0xf59bdc1e08324a76,
+     0x23a4c608f19be5d7, 0x024537e61f89abcd, 0x71234560a9bcdef8, 0x801264579ac3bdef),
+    (0x3b791efd20c8645a, 0xb5179fd3ca068e42, 0xa2917d35fcb4e860, 0xf7b0d354a21e968c,
+     0x790b364fd12ca5e8, 0x23a567e10b894fcd, 0x1023456789abcdfe, 0x01325476e89abcdf),
 )
-APART = 2
+APART = 4
 
 
 def owner_table():

time: 58.6 us -> 58.2 us (level)
  Pallas kernels: 5.65 us -> 6.96 us
  blocking collectives: 33.4 us -> 32.6 us
  starting transfers between devices: 14.2 us -> 13.5 us
    all_to_all x1, blocking collectives: 20.8 us -> 18.6 us  [body(): rows = lax.all_to_all(column_call(rows), PLANE, 0, 0, tiled=True)]
    ppermute x1, starting transfers between devices: 12.3 us -> 10.2 us  [body(): two = lax.ppermute(sent, AXES, far)]
    all_to_all x1, blocking collectives: 12.5 us -> 14 us  [body(): rows = lax.all_to_all(rows, STACK, 0, 0, tiled=True)]
    ppermute x1, starting transfers between devices: 1.92 us -> 3.35 us  [body(): one = lax.ppermute(sent, AXES, near)]
    pallas_call x1, Pallas kernels: 1.8 us -> 2.56 us  [prep_call(): pl.pallas_call(prep_kernel, out_shape=(pltpu.VMEM((2, occupied * width_bl...]
  transfers between devices with their start and end apart: 2 -> 2, of which waited for: 1 -> 1; matrix products, arithmetic and copies ran while one was open for 0% -> 0% of each run, Pallas kernels for 3% -> 4%
where the time goes in v7:
time: 58.2 us; the launch traced here: 57.8 us
  blocking collectives  32.6 us (56%)
  starting transfers between devices  13.5 us (23%)
  Pallas kernels  6.96 us (12%)
  waiting for transfers between devices  3.43 us (6%)
  between operations  1.33 us (2%)
    all_to_all x1, blocking collectives, body(): rows = lax.all_to_all(column_call(rows), PLANE, 0, 0, tiled=True)  18.6 us
    all_to_all x1, blocking collectives, body(): rows = lax.all_to_all(rows, STACK, 0, 0, tiled=True)  14 us
    ppermute x1, starting transfers between devices, body(): two = lax.ppermute(sent, AXES, far)  10.2 us
    ppermute x1, waiting for transfers between devices, body(): one = lax.ppermute(sent, AXES, near)  3.43 us
    ppermute x1, starting transfers between devices, body(): one = lax.ppermute(sent, AXES, near)  3.35 us
    pallas_call x1, Pallas kernels, energy_call(): pl.pallas_call(energy_kernel, out_shape=pltpu.VMEM((32, 128), F32), in_sp...  2.68 us
    pallas_call x1, Pallas kernels, prep_call(): pl.pallas_call(prep_kernel, out_shape=(pltpu.VMEM((2, occupied * width_bl...  2.56 us
  transfers between devices with their start and end apart: 2, of which 1 were waited for; matrix products, arithmetic and copies ran while one was open for 0% of the time, Pallas kernels for 4%

profile of v7, /device:TPU:1, one launch (start us, length us, event | category | flops | bytes accessed | tf_op | source)
XLA Modules:
  0.0 57.8 jit_solution(12398338389446781114)
XLA Ops:
  0.6 0.8 %rows.1 = bf16[2,128,128]{2,1,0:T(8,128)(2,1)S(1)} custom-call(bf16[4,128,128]{2,1,0:T(8,128)(2,1)} %doubles_ref.1, bf16[4,128,128]{2,1,0:T(8,128)(2,1)} %coulomb_ref.1), custom_call_target="tpu_custom_call" | custom-call | flops 1000000000 | bytes 1048576 | tf_op jit(solution)/shard_map/rows/pallas_call | solution.py:266
  1.4 10.2 %collective-permute-start.1 = (bf16[2,128,128]{2,1,0:T(8,128)(2,1)S(1)}, bf16[2,128,128]{2,1,0:T(8,128)(2,1)S(1)}, u32[]{:S(2)}, u32[]{:S(2)}) collective-permute-start(bf16[2,128,128]{2,1,0:T(8,128)(2,1)S(1)} %rows.1), channel_id=1, source_target_pairs={{520,0},{525,1},{526,2},{524,3},{521,4},{527,5},{523,6},{522,7},{5... | collective-permute-start | bytes 196616 | tf_op jit(solution)/shard_map/ppermute | solution.py:338
  11.6 3.3 %collective-permute-start = (bf16[2,128,128]{2,1,0:T(8,128)(2,1)S(1)}, bf16[2,128,128]{2,1,0:T(8,128)(2,1)S(1)}, u32[]{:S(2)}, u32[]{:S(2)}) collective-permute-start(bf16[2,128,128]{2,1,0:T(8,128)(2,1)S(1)} %rows.1), channel_id=1, source_target_pairs={{1,0},{521,1},{7,2},{5,3},{525,4},{523,5},{527,6},{3,7},{14,8},{51... | collective-permute-start | bytes 196616 | tf_op jit(solution)/shard_map/ppermute | solution.py:339
  15.6 0.0 copy-start
  15.6 2.6 %prep.1 = (f32[2,64,128,128]{3,2,1,0:T(8,128)S(1)}, f32[64,128]{1,0:T(8,128)S(1)}, f32[1,128]{1,0:T(1,128)S(1)}, f32[1,128]{1,0:T(1,128)S(1)}, f32[4,16,128]{2,1,0:T(8,128)S(1)}) custom-call(s32[512]{0:T(512)} %constant.2.clone.owners_ref, s32[3,1,16]{2,1,0:T(1,128)} %bitcast.11, s32[1]{0:T(128)S(6)} %copy.11.count_ref, f32[8]{0:T(128)} %occ_ref.1, ...), custom_call_target="tpu_custom_call" | custom-call | flops 10000000000 | bytes 16777216 | tf_op jit(solution)/shard_map/prep/pallas_call | solution.py:282
  18.2 0.0 collective-permute-done.1.two_ref
  18.2 3.4 %collective-permute-done.one_ref = bf16[2,128,128]{2,1,0:T(8,128)(2,1)S(1)} collective-permute-done((bf16[2,128,128]{2,1,0:T(8,128)(2,1)S(1)}, bf16[2,128,128]{2,1,0:T(8,128)(2,1)S(1)}, u32[]{:S(2)}, u32[]{:S(2)}) %collective-permute-start) | collective-permute-done | bytes 65568 | tf_op jit(solution)/shard_map/ppermute | solution.py:339
  21.6 0.0 copy-done
  21.6 2.7 %energies.1 = f32[32,128]{1,0:T(8,128)S(1)} custom-call(bf16[8,8,128,128]{3,2,1,0:T(8,128)(2,1)S(1)} %copy-done, bf16[2,128,128]{2,1,0:T(8,128)(2,1)S(1)} %collective-permute-done.one_ref, bf16[2,128,128]{2,1,0:T(8,128)(2,1)S(1)} %collective-permute-done.1.two_ref, f32[2,64,128,128]{3,2,1,0:T(8,128)S(1)} %get-tuple-element.9.recip_ref, ...), custom_call_target="tpu_custom_call" | custom-call | tf_op jit(solution)/shard_map/energies/pallas_call | solution.py:301
  24.3 14.0 %all_to_all.22 = f32[16,2,128]{2,1,0:T(2,128)S(1)} all-to-all(f32[16,2,128]{2,1,0:T(2,128)S(1)} %bitcast.9), channel_id=1, replica_groups=mesh['yl'=4,'z'=8,'c'=2,'yh'=2,'x'=8] {'z','c'}, dimensions={0} | all-to-all | bytes 32768 | tf_op jit(solution)/shard_map/all_to_all | solution.py:343
  38.3 18.6 %all_to_all.23 = f32[64,2,128]{2,1,0:T(2,128)S(1)} all-to-all(f32[64,2,128]{2,1,0:T(2,128)S(1)} %bitcast.7), channel_id=1, replica_groups=mesh['yl'=4,'z'=8,'c'=2,'yh'=2,'x'=8] {'yh','yl','x'}, dimensions={0} | all-to-all | bytes 131072 | tf_op jit(solution)/shard_map/all_to_all | solution.py:344
  56.9 0.9 %lookup.1 = (f32[1,16]{1,0:T(1,128)}, f32[1,1]{1,0:T(1,128)}) custom-call(f32[128,128]{1,0:T(8,128)S(1)} %bitcast.8, f32[4,16,128]{2,1,0:T(8,128)S(1)} %get-tuple-element.13.slots_ref), custom_call_target="tpu_custom_call" | custom-call | tf_op jit(solution)/shard_map/lookup/pallas_call | solution.py:325
  (1 shorter events, 0.0 us)
Async XLA Ops:
  1.4 16.8 %collective-permute-start.1 = (bf16[2,128,128]{2,1,0:T(8,128)(2,1)S(1)}, bf16[2,128,128]{2,1,0:T(8,128)(2,1)S(1)}, u32[]{:S(2)}, u32[]{:S(2)}) collective-permute-start(bf16[2,128,128]{2,1,0:T(8,128)(2,1)S(1)} %rows.1), channel_id=1, source_target_pairs={{520,0},{525,1},{526,2},{524,3},{521,4},{527,5},{523,6},{522,7},{5... | collective-permute-start | bytes 196616 | tf_op jit(solution)/shard_map/ppermute | solution.py:338
  11.6 10.0 %collective-permute-start = (bf16[2,128,128]{2,1,0:T(8,128)(2,1)S(1)}, bf16[2,128,128]{2,1,0:T(8,128)(2,1)S(1)}, u32[]{:S(2)}, u32[]{:S(2)}) collective-permute-start(bf16[2,128,128]{2,1,0:T(8,128)(2,1)S(1)} %rows.1), channel_id=1, source_target_pairs={{1,0},{521,1},{7,2},{5,3},{525,4},{523,5},{527,6},{3,7},{14,8},{51... | collective-permute-start | bytes 196616 | tf_op jit(solution)/shard_map/ppermute | solution.py:339
  15.6 6.0 %copy-start = (bf16[8,8,128,128]{3,2,1,0:T(8,128)(2,1)S(1)}, bf16[8,8,128,128]{3,2,1,0:T(8,128)(2,1)}, u32[]{:S(2)}) copy-start(bf16[8,8,128,128]{3,2,1,0:T(8,128)(2,1)} %ints_ref.1) | copy-start | bytes 6291460
